TPU v7x, 32 devices: a whole 2x2x4 slice. The times are simulated.
32 devices in a mesh: dp: 4 (over x, core), seq: 8 (over z, y).
Axes of the slice: x: 2, y: 2, z: 4, core: 2. Of those that a mesh axis runs over, the one named last changes fastest.
Arguments:
- block_input: bfloat16 [4, 1024, 2048], P('dp', 'seq'), may hold values from -6 to 6
- norm_gain: bfloat16 [2048], P(('dp', 'seq')), may hold values from 0.5 to 1.5
- in_weight: bfloat16 [2048, 8192], P(('dp', 'seq')), may hold values from -0.125 to 0.125
- conv_weight: bfloat16 [4096, 4], P(('dp', 'seq')), may hold values from -3 to 3
- conv_bias: bfloat16 [4096], P(('dp', 'seq')), may hold values from -3 to 3
- select_weight: bfloat16 [4096, 160], P(('dp', 'seq')), may hold values from -0.09375 to 0.09375
- step_weight: bfloat16 [4096, 128], P(('dp', 'seq')), may hold values from -0.5 to 0.5
- step_bias: bfloat16 [4096], P(('dp', 'seq')), may hold values from -7 to -2.25
- decay_log: bfloat16 [4096, 16], P(('dp', 'seq')), may hold values from -3 to 2.765625
- skip_gain: bfloat16 [4096], P(('dp', 'seq')), may hold values from 0.5 to 1.5
- out_weight: bfloat16 [4096, 2048], P(('dp', 'seq')), may hold values from -0.1875 to 0.1875
- output_grad: bfloat16 [4, 1024, 2048], P('dp', 'seq'), may hold values from -6 to 6
Outputs:
- layer_output: bfloat16 [4, 1024, 2048], P('dp', 'seq')
- input_grad: bfloat16 [4, 1024, 2048], P('dp', 'seq')
- grad_norm_gain: float32 [2048], P(('dp', 'seq'))
- grad_in_weight: float32 [2048, 8192], P(('dp', 'seq'))
- grad_conv_weight: float32 [4096, 4], P(('dp', 'seq'))
- grad_conv_bias: float32 [4096], P(('dp', 'seq'))
- grad_select_weight: float32 [4096, 160], P(('dp', 'seq'))
- grad_step_weight: float32 [4096, 128], P(('dp', 'seq'))
- grad_step_bias: float32 [4096], P(('dp', 'seq'))
- grad_decay_log: float32 [4096, 16], P(('dp', 'seq'))
- grad_skip_gain: float32 [4096], P(('dp', 'seq'))
- grad_out_weight: float32 [4096, 2048], P(('dp', 'seq'))
All inputs are finite; a program needn't handle non-finite values.
Results may differ from a plain program's by a relative error of at most 0.012.
Values may be sent and summed in bfloat16 or wider, within the bound.
A program may use at most 320 MiB of HBM per device.

v0:
```python
import jax
import jax.numpy as jnp
from jax import lax
from jax.sharding import PartitionSpec as P

STATE = 16
RANK = 128
KERNEL = 4


EPS = 1e-05


def from_behind(value, axis, steps):
    count = lax.axis_size(axis)
    first, last = (max(0, -steps), min(count, count - steps))
    return lax.ppermute(value, axis, [(source, source + steps) for source in range(first, last)])


def carried_in(part, axis, combine, identity, reverse):
    count = lax.axis_size(axis)
    place = lax.axis_index(axis)
    ahead = count - 1 - place if reverse else place
    gathered = jax.tree.map(lambda a: lax.all_gather(a, axis), part)
    state = jax.tree.map(lambda a, e: jnp.zeros_like(a) + jnp.asarray(e, a.dtype), part, identity)

    def one(turn, state):
        source = count - 1 - turn if reverse else turn
        return combine(
            state, jax.tree.map(lambda a: lax.dynamic_index_in_dim(a, source, 0, False), gathered)
        )

    return lax.fori_loop(0, ahead, one, state)


def silu_slope(values_in):
    sigmoid_value = jax.nn.sigmoid(values_in)
    return sigmoid_value * (1.0 + values_in * (1.0 - sigmoid_value))


def run_block(carry_state, inner_blk, delta_blk, write_blk, read_blk, decay_rate):
    outputs = []
    for position in range(inner_blk.shape[0]):
        delta_now = delta_blk[position]
        carry_state = (
            jnp.exp(delta_now[None, :] * decay_rate) * carry_state
            + write_blk[position][:, None] * (delta_now * inner_blk[position])[None, :]
        )
        outputs.append(jnp.sum(carry_state * read_blk[position][:, None], axis=0))
    return (jnp.stack(outputs), carry_state)


def run_chain(start_state, pieces, decay_rate):

    def advance(carry_state, blocked_in):
        block_out, next_state = run_block(
            carry_state, blocked_in[0], blocked_in[1], blocked_in[2], blocked_in[3], decay_rate
        )
        return (next_state, (block_out, carry_state))

    return lax.scan(advance, start_state, pieces)


def link_states(earlier, latter):
    return (earlier[0] * latter[0], latter[0] * earlier[1] + latter[1])


def to_blocks(values_in):
    return values_in.reshape(16, values_in.shape[0] // 16, values_in.shape[1])


def from_blocks(values_in):
    return values_in.reshape(values_in.shape[0] * values_in.shape[1], values_in.shape[2])


def decayed_rows(cumulative, read_vec, incoming, decay_rate):
    length = cumulative.shape[0]
    rows = min(128, length)
    blocks = length // rows

    def one_block(blocked):
        cum_blk, read_blk = blocked
        return jnp.sum(
            jnp.exp(cum_blk[:, None, :] * decay_rate[None]) * read_blk[:, :, None] * incoming[None],
            axis=1,
        )

    result = lax.map(
        one_block,
        (
            cumulative.reshape(blocks, rows, cumulative.shape[1]),
            read_vec.reshape(blocks, rows, read_vec.shape[1]),
        ),
    )
    return result.reshape(length, cumulative.shape[1])


def decayed_total(cumulative, read_vec, grad_scan, decay_rate):
    length = cumulative.shape[0]
    rows = min(128, length)
    blocks = length // rows

    def one_block(total, blocked):
        cum_blk, read_blk, grad_blk = blocked
        return (
            total
            + jnp.sum(
                jnp.exp(cum_blk[:, None, :] * decay_rate[None])
                * read_blk[:, :, None]
                * grad_blk[:, None, :],
                axis=0,
            ),
            None,
        )

    total, unused_rest = lax.scan(
        one_block,
        jnp.zeros(decay_rate.shape, jnp.float32),
        (
            cumulative.reshape(blocks, rows, cumulative.shape[1]),
            read_vec.reshape(blocks, rows, read_vec.shape[1]),
            grad_scan.reshape(blocks, rows, grad_scan.shape[1]),
        ),
    )
    return total


def front_half(token_rows, weights):
    norm_scale = weights[0].astype(jnp.float32)
    mean_sq = jnp.mean(token_rows * token_rows, axis=1, keepdims=True)
    row_scale = lax.rsqrt(mean_sq + EPS)
    normed = (token_rows * row_scale * norm_scale).astype(jnp.bfloat16)
    mixed = jnp.dot(normed, weights[1], preferred_element_type=jnp.float32).astype(jnp.bfloat16)
    return (row_scale, normed, mixed)


def mixer_pieces(mixed, prior_rows, weights):
    inner_width = mixed.shape[1] // 2
    length = mixed.shape[0]
    padded = jnp.concatenate([prior_rows, mixed[:, :inner_width]], axis=0).astype(jnp.float32)
    conv_taps = weights[2].astype(jnp.float32).T
    conv_out = weights[3].astype(jnp.float32) + jnp.zeros((length, inner_width), jnp.float32)
    for offset in range(KERNEL):
        conv_out = conv_out + padded[offset : offset + length] * conv_taps[offset]
    inner_act = jax.nn.silu(conv_out).astype(jnp.bfloat16)
    picked = jnp.dot(inner_act, weights[4], preferred_element_type=jnp.float32).astype(jnp.bfloat16)
    step_in = picked[:, :RANK]
    write_vec = picked[:, RANK : RANK + STATE].astype(jnp.float32)
    read_vec = picked[:, RANK + STATE :].astype(jnp.float32)
    step_raw = lax.dot_general(
        step_in, weights[5], (((1,), (1,)), ((), ())), preferred_element_type=jnp.float32
    ) + weights[6].astype(jnp.float32)
    step_size = jax.nn.softplus(step_raw)
    decay_rate = -jnp.exp(weights[7].astype(jnp.float32).T)
    return (
        padded,
        conv_out,
        inner_act,
        picked,
        step_raw,
        step_size,
        decay_rate,
        write_vec,
        read_vec,
    )


def shards(
    block_input,
    norm_gain,
    in_weight,
    conv_weight,
    conv_bias,
    select_weight,
    step_weight,
    step_bias,
    decay_log,
    skip_gain,
    out_weight,
    output_grad,
):
    weights = (
        lax.all_gather(norm_gain, ("dp", "seq"), axis=0, tiled=True),
        lax.all_gather(in_weight, ("dp", "seq"), axis=0, tiled=True),
        lax.all_gather(conv_weight, ("dp", "seq"), axis=0, tiled=True),
        lax.all_gather(conv_bias, ("dp", "seq"), axis=0, tiled=True),
        lax.all_gather(select_weight, ("dp", "seq"), axis=0, tiled=True),
        lax.all_gather(step_weight, ("dp", "seq"), axis=0, tiled=True),
        lax.all_gather(step_bias, ("dp", "seq"), axis=0, tiled=True),
        lax.all_gather(decay_log, ("dp", "seq"), axis=0, tiled=True),
        lax.all_gather(skip_gain, ("dp", "seq"), axis=0, tiled=True),
        lax.all_gather(out_weight, ("dp", "seq"), axis=0, tiled=True),
    )
    token_rows = block_input[0].astype(jnp.float32)
    length = token_rows.shape[0]
    inner_width = in_weight.shape[1] // 2
    row_scale, normed, mixed = front_half(token_rows, weights)
    prior_rows = from_behind(mixed[length - (KERNEL - 1) :, :inner_width], "seq", 1)
    padded, conv_out, inner_act, picked, step_raw, step_size, decay_rate, write_vec, read_vec = (
        mixer_pieces(mixed, prior_rows, weights)
    )
    inner_f = inner_act.astype(jnp.float32)
    pieces = (to_blocks(inner_f), to_blocks(step_size), to_blocks(write_vec), to_blocks(read_vec))
    local_end, (local_out, unused_starts) = run_chain(
        jnp.zeros(decay_rate.shape, jnp.float32), pieces, decay_rate
    )
    cumulative = jnp.cumsum(step_size, axis=0)
    carried = jnp.exp(decay_rate * cumulative[length - 1][None, :])
    incoming = carried_in(
        (carried, local_end),
        "seq",
        link_states,
        (jnp.ones_like(carried), jnp.zeros_like(local_end)),
        False,
    )[1]
    correction = decayed_rows(cumulative, read_vec, incoming, decay_rate)
    skip_scale = weights[8].astype(jnp.float32)
    gate_in = mixed[:, inner_width:].astype(jnp.float32)
    mamba_out = from_blocks(local_out) + correction + skip_scale * inner_f
    gated_out = (mamba_out * jax.nn.silu(gate_in)).astype(jnp.bfloat16)
    layer_out = token_rows + jnp.dot(gated_out, weights[9], preferred_element_type=jnp.float32)
    back_weights = (
        lax.all_gather(norm_gain, ("dp", "seq"), axis=0, tiled=True),
        lax.all_gather(in_weight, ("dp", "seq"), axis=0, tiled=True),
        lax.all_gather(conv_weight, ("dp", "seq"), axis=0, tiled=True),
        lax.all_gather(conv_bias, ("dp", "seq"), axis=0, tiled=True),
        lax.all_gather(select_weight, ("dp", "seq"), axis=0, tiled=True),
        lax.all_gather(step_weight, ("dp", "seq"), axis=0, tiled=True),
        lax.all_gather(step_bias, ("dp", "seq"), axis=0, tiled=True),
        lax.all_gather(decay_log, ("dp", "seq"), axis=0, tiled=True),
        lax.all_gather(skip_gain, ("dp", "seq"), axis=0, tiled=True),
        lax.all_gather(out_weight, ("dp", "seq"), axis=0, tiled=True),
    )
    row_scale, normed, mixed = front_half(token_rows, back_weights)
    padded, conv_out, inner_act, picked, step_raw, step_size, decay_rate, write_vec, read_vec = (
        mixer_pieces(mixed, prior_rows, back_weights)
    )
    inner_f = inner_act.astype(jnp.float32)
    pieces = (to_blocks(inner_f), to_blocks(step_size), to_blocks(write_vec), to_blocks(read_vec))
    unused_end, (true_out, block_starts) = run_chain(incoming, pieces, decay_rate)
    skip_scale = back_weights[8].astype(jnp.float32)
    gate_in = mixed[:, inner_width:].astype(jnp.float32)
    gate_act = jax.nn.silu(gate_in)
    mamba_out = from_blocks(true_out) + skip_scale * inner_f
    gated_out = (mamba_out * gate_act).astype(jnp.bfloat16)
    upstream = output_grad[0]
    grad_gated = lax.dot_general(
        upstream, back_weights[9], (((1,), (1,)), ((), ())), preferred_element_type=jnp.float32
    )
    grad_out_weight = lax.dot_general(
        gated_out, upstream, (((0,), (0,)), ((), ())), preferred_element_type=jnp.float32
    )
    grad_scan = grad_gated * gate_act
    grad_gate = grad_gated * mamba_out * silu_slope(gate_in)
    grad_skip = jnp.sum(grad_scan * inner_f, axis=0)
    cumulative = jnp.cumsum(step_size, axis=0)
    direct = decayed_total(cumulative, read_vec, grad_scan, decay_rate)
    carried = jnp.exp(decay_rate * cumulative[length - 1][None, :])
    arriving = carried_in(
        (carried, direct),
        "seq",
        link_states,
        (jnp.ones_like(carried), jnp.zeros_like(direct)),
        True,
    )[1]

    def retreat(carry_in, blocked_in):
        grad_state, grad_decay = carry_in
        block_start, inner_blk, delta_blk, write_blk, read_blk, out_blk = blocked_in
        unused_primal, pullback = jax.vjp(
            run_block, block_start, inner_blk, delta_blk, write_blk, read_blk, decay_rate
        )
        block_grads = pullback((out_blk, grad_state))
        return (
            (block_grads[0], grad_decay + block_grads[5]),
            (block_grads[1], block_grads[2], block_grads[3], block_grads[4]),
        )

    (unused_state, grad_decay), (back_inner, back_delta, back_write, back_read) = lax.scan(
        retreat,
        (arriving, jnp.zeros_like(decay_rate)),
        (block_starts,) + pieces + (to_blocks(grad_scan),),
        reverse=True,
    )
    grad_raw_f = from_blocks(back_delta) * jax.nn.sigmoid(step_raw)
    grad_step_bias = jnp.sum(grad_raw_f, axis=0)
    grad_raw = grad_raw_f.astype(jnp.bfloat16)
    step_in = picked[:, :RANK]
    grad_step_weight = lax.dot_general(
        grad_raw, step_in, (((0,), (0,)), ((), ())), preferred_element_type=jnp.float32
    )
    grad_step_in = jnp.dot(grad_raw, back_weights[5], preferred_element_type=jnp.float32)
    grad_picked = jnp.concatenate(
        [grad_step_in, from_blocks(back_write), from_blocks(back_read)], axis=1
    ).astype(jnp.bfloat16)
    grad_select = lax.dot_general(
        inner_act, grad_picked, (((0,), (0,)), ((), ())), preferred_element_type=jnp.float32
    )
    grad_inner = (
        from_blocks(back_inner)
        + grad_scan * skip_scale
        + lax.dot_general(
            grad_picked,
            back_weights[4],
            (((1,), (1,)), ((), ())),
            preferred_element_type=jnp.float32,
        )
    )
    grad_conv = grad_inner * silu_slope(conv_out)
    grad_conv_bias = jnp.sum(grad_conv, axis=0)
    conv_taps = back_weights[2].astype(jnp.float32).T
    grad_taps = jnp.stack(
        [jnp.sum(grad_conv * padded[offset : offset + length], axis=0) for offset in range(KERNEL)],
        axis=1,
    )
    extended = jnp.pad(grad_conv, ((KERNEL - 1, KERNEL - 1), (0, 0)))
    grad_padded = jnp.zeros((length + KERNEL - 1, inner_width), jnp.float32)
    for offset in range(KERNEL):
        begin = KERNEL - 1 - offset
        grad_padded = (
            grad_padded + extended[begin : begin + length + KERNEL - 1] * conv_taps[offset]
        )
    returned = from_behind(grad_padded[: KERNEL - 1].astype(jnp.bfloat16), "seq", -1).astype(
        jnp.float32
    )
    grad_conv_in = grad_padded[KERNEL - 1 :] + jnp.concatenate(
        [jnp.zeros((length - (KERNEL - 1), inner_width), jnp.float32), returned], axis=0
    )
    grad_mixed = jnp.concatenate([grad_conv_in, grad_gate], axis=1).astype(jnp.bfloat16)
    grad_in_weight = lax.dot_general(
        normed, grad_mixed, (((0,), (0,)), ((), ())), preferred_element_type=jnp.float32
    )
    grad_normed = lax.dot_general(
        grad_mixed, back_weights[1], (((1,), (1,)), ((), ())), preferred_element_type=jnp.float32
    )
    norm_scale = back_weights[0].astype(jnp.float32)
    grad_gain = jnp.sum(grad_normed * token_rows * row_scale, axis=0)
    scaled_grad = grad_normed * norm_scale
    grad_rows = row_scale * scaled_grad - token_rows * row_scale * row_scale * row_scale * jnp.mean(
        scaled_grad * token_rows, axis=1, keepdims=True
    )
    input_grad = (upstream.astype(jnp.float32) + grad_rows).astype(jnp.bfloat16)
    grad_decay_log = (grad_decay * decay_rate).T
    summed = (
        lax.psum_scatter(grad_gain, ("dp", "seq"), scatter_dimension=0, tiled=True),
        lax.psum_scatter(grad_in_weight, ("dp", "seq"), scatter_dimension=0, tiled=True),
        lax.psum_scatter(grad_taps, ("dp", "seq"), scatter_dimension=0, tiled=True),
        lax.psum_scatter(grad_conv_bias, ("dp", "seq"), scatter_dimension=0, tiled=True),
        lax.psum_scatter(grad_select, ("dp", "seq"), scatter_dimension=0, tiled=True),
        lax.psum_scatter(grad_step_weight, ("dp", "seq"), scatter_dimension=0, tiled=True),
        lax.psum_scatter(grad_step_bias, ("dp", "seq"), scatter_dimension=0, tiled=True),
        lax.psum_scatter(grad_decay_log, ("dp", "seq"), scatter_dimension=0, tiled=True),
        lax.psum_scatter(grad_skip, ("dp", "seq"), scatter_dimension=0, tiled=True),
        lax.psum_scatter(grad_out_weight, ("dp", "seq"), scatter_dimension=0, tiled=True),
    )
    return (
        layer_out.astype(jnp.bfloat16)[None],
        input_grad[None],
        summed[0],
        summed[1],
        summed[2],
        summed[3],
        summed[4],
        summed[5],
        summed[6],
        summed[7],
        summed[8],
        summed[9],
    )


def solution(mesh):
    return jax.shard_map(
        shards,
        mesh=mesh,
        in_specs=(
            P("dp", "seq", None),
            P(("dp", "seq")),
            P(("dp", "seq"), None),
            P(("dp", "seq"), None),
            P(("dp", "seq")),
            P(("dp", "seq"), None),
            P(("dp", "seq"), None),
            P(("dp", "seq")),
            P(("dp", "seq"), None),
            P(("dp", "seq")),
            P(("dp", "seq"), None),
            P("dp", "seq", None),
        ),
        out_specs=(
            P("dp", "seq", None),
            P("dp", "seq", None),
            P(("dp", "seq")),
            P(("dp", "seq"), None),
            P(("dp", "seq"), None),
            P(("dp", "seq")),
            P(("dp", "seq"), None),
            P(("dp", "seq"), None),
            P(("dp", "seq")),
            P(("dp", "seq"), None),
            P(("dp", "seq")),
            P(("dp", "seq"), None),
        ),
        check_vma=False,
    )
```

profile of v0, /device:TPU:12, one launch (start us, length us, event | category | flops | bytes accessed | tf_op | source)
XLA Modules:
  0.0 3601.7 jit_solution(9255164238112288245)
XLA Ops:
  10.9 43.6 %all-reduce.34 = bf16[2048]{0:T(1024)(128)(2,1)S(1)} all-reduce(bf16[2048]{0:T(1024)(128)(2,1)S(1)} %dynamic-update-slice), channel_id=1, replica_groups=mesh['dp'=4,'seq'=8] {'dp','seq'}, use_global_device_ids=true, to_apply=%add.34 | all-reduce | flops 2048 | bytes 8192
  55.9 63.8 %all_gather.63 = bf16[4096,4]{0,1:T(4,128)(2,1)S(1)} all-gather(bf16[128,4]{0,1:T(4,128)(2,1)S(1)} %copy-done.30), channel_id=1, replica_groups=mesh['dp'=4,'seq'=8] {'dp','seq'}, dimensions={0}, use_global_device_ids=true | all-gather | bytes 33792 | tf_op jit(solution)/shard_map/all_gather | solution.py:185
  119.7 69.4 %all_gather.67 = bf16[4096,16]{0,1:T(8,128)(2,1)S(1)} all-gather(bf16[128,16]{0,1:T(8,128)(2,1)S(1)} %copy-done.29), channel_id=1, replica_groups=mesh['dp'=4,'seq'=8] {'dp','seq'}, dimensions={0}, use_global_device_ids=true | all-gather | bytes 135168 | tf_op jit(solution)/shard_map/all_gather | solution.py:190
  189.2 17.9 all-gather.14.cloned.1.call-done
  207.1 15.2 convolution_convert_fusion
  222.3 5.3 collective-permute-start
  227.7 63.7 %all-gather.3 = bf16[32,1,128]{2,1,0:T(2,128)(2,1)S(1)} all-gather(bf16[1,1,128]{2,1,0:T(2,128)(2,1)S(1)} %bitcast.853), channel_id=1, replica_groups=mesh['dp'=4,'seq'=8] {'dp','seq'}, dimensions={0}, use_global_device_ids=true | all-gather | bytes 8448 | tf_op jit(solution)/shard_map/all_gather | solution.py:186
  291.4 64.7 %all-gather.4 = bf16[32,1,128]{2,1,0:T(2,128)(2,1)S(1)} all-gather(bf16[1,1,128]{2,1,0:T(2,128)(2,1)S(1)} %bitcast.854), channel_id=1, replica_groups=mesh['dp'=4,'seq'=8] {'dp','seq'}, dimensions={0}, use_global_device_ids=true | all-gather | bytes 8448 | tf_op jit(solution)/shard_map/all_gather | solution.py:189
  357.9 14.9 fusion.19
  372.8 3.5 all-gather.16.cloned.1.call-done
  379.8 52.1 %all-gather.18.cloned.1.call-done = bf16[4096,128]{1,0:T(8,128)(2,1)} async-done(((bf16[128,128]{1,0:T(8,128)(2,1)}), bf16[4096,128]{1,0:T(8,128)(2,1)}) %all-gather.18.cloned.1.call-update) | async-done | bytes 1048592 | tf_op jit(solution)/shard_map/all_gather | solution.py:188
  433.7 3.1 fusion.63
  436.8 4.6 reduce_window_sum.12
  444.8 73.5 %while.89 = (s32[]{:T(128)}, f32[16,4096]{1,0:T(8,128)S(1)}, f32[16,8,4096]{2,1,0:T(8,128)}, f32[16,8,4096]{2,1,0:T(8,128)}, f32[16,4096]{1,0:T(8,128)S(1)}, /*i...) while((s32[]{:T(128)}, f32[16,4096]{1,0:T(8,128)S(1)}, ...), condition=%wide.region_10.11_spmd.clone, body=%wide.region_1.10_spmd.clone.sunk | while | flops 4587530 | bytes 5150316 | solution.py:61
  444.9 2.4 constant_dynamic-slice_fusion.74
  449.5 2.6 constant_dynamic-slice_fusion.74
  454.3 2.6 constant_dynamic-slice_fusion.74
  459.1 2.3 constant_dynamic-slice_fusion.74
  463.6 2.4 constant_dynamic-slice_fusion.74
  468.2 2.4 constant_dynamic-slice_fusion.74
  472.8 2.3 constant_dynamic-slice_fusion.74
  477.3 2.4 constant_dynamic-slice_fusion.74
  481.9 2.3 constant_dynamic-slice_fusion.74
  486.4 2.5 constant_dynamic-slice_fusion.74
  491.2 2.3 constant_dynamic-slice_fusion.74
  495.7 2.3 constant_dynamic-slice_fusion.74
  500.2 2.7 constant_dynamic-slice_fusion.74
  509.4 2.4 constant_dynamic-slice_fusion.74
  514.0 2.2 constant_dynamic-slice_fusion.74
  519.2 63.1 %all-gather.5 = bf16[32,1,128]{2,1,0:T(2,128)(2,1)S(1)} all-gather(bf16[1,1,128]{2,1,0:T(2,128)(2,1)S(1)} %bitcast.855), channel_id=1, replica_groups=mesh['dp'=4,'seq'=8] {'dp','seq'}, dimensions={0}, use_global_device_ids=true | all-gather | bytes 8448 | tf_op jit(solution)/shard_map/all_gather | solution.py:191
  582.4 3.6 while.86
  585.9 15.3 multiply_reduce_fusion.48
  603.2 85.4 %while.88 = (s32[]{:T(128)}, f32[16,4096]{1,0:T(8,128)S(1)}, f32[16,8,4096]{2,1,0:T(8,128)}, f32[16,16,4096]{2,1,0:T(8,128)}, f32[16,8,4096]{2,1,0:T(8,128)}, /*...) while((s32[]{:T(128)}, f32[16,4096]{1,0:T(8,128)S(1)}, ...), condition=%wide.region_27.28_spmd, body=%wide.region_18.27_spmd.sunk | while | flops 4718601 | bytes 4658861 | solution.py:61
  603.9 2.4 constant_dynamic-slice_fusion.72
  609.3 2.6 constant_dynamic-slice_fusion.72
  614.9 2.6 constant_dynamic-slice_fusion.72
  620.4 2.3 constant_dynamic-slice_fusion.72
  625.7 2.4 constant_dynamic-slice_fusion.72
  631.0 2.4 constant_dynamic-slice_fusion.72
  636.4 2.3 constant_dynamic-slice_fusion.72
  641.6 2.4 constant_dynamic-slice_fusion.72
  647.0 2.3 constant_dynamic-slice_fusion.72
  652.2 2.5 constant_dynamic-slice_fusion.72
  657.7 2.3 constant_dynamic-slice_fusion.72
  663.0 2.3 constant_dynamic-slice_fusion.72
  668.2 2.7 constant_dynamic-slice_fusion.72
  678.9 2.4 constant_dynamic-slice_fusion.72
  684.2 2.2 constant_dynamic-slice_fusion.72
  688.6 4.7 while.87
  696.5 221.1 %while.90 = (s32[]{:T(128)}, f32[16,4096]{1,0:T(8,128)S(1)}, f32[16,4096]{1,0:T(8,128)S(1)}, f32[16,8,4096]{2,1,0:T(8,128)}, f32[16,8,4096]{2,1,0:T(8,128)}, /*i...) while((s32[]{:T(128)}, f32[16,4096]{1,0:T(8,128)S(1)}, ...), condition=%wide.region_61.62_spmd.clone, body=%wide.region_28.61_spmd.clone.sunk | while | flops 17171980 | bytes 12148675 | solution.py:279
  917.7 3.0 fusion.65
  922.4 5.0 multiply_reduce_fusion.53
  935.9 17.1 fusion.38
  953.8 4.6 multiply_add_fusion.29
  958.5 4.3 collective-permute-start.1
  966.5 23.4 fusion.28
  991.5 10.7 fusion.16
  1002.3 18.9 fusion.42
  1021.2 44.3 %all-reduce.39 = (f32[2048]{0:T(1024)S(1)}, f32[4096]{0:T(1024)S(1)}, f32[4096]{0:T(1024)S(1)}, f32[4096]{0:T(1024)S(1)}) all-reduce(f32[2048]{0:T(1024)S(1)} %get-tuple-element.716, f32[4096]{0:T(1024)S(1)} %get-tuple-element.715, f32[4096]{0:T(1024)S(1)} %get-tuple-element.820, ...), channel_id=5, replica_groups=mesh['dp'=4,'seq'=8] {'dp','seq'}, use_global_device_ids=true, to_apply=%region_64.65.clone | all-reduce | flops 14336 | bytes 114688
  1070.6 128.8 %reduce-scatter.15.cloned.1.call-done = f32[128,16]{0,1:T(8,128)} async-done(((f32[4096,16]{0,1:T(8,128)}), f32[128,16]{0,1:T(8,128)}) %reduce-scatter.15.cloned.1.call-update) | async-done | bytes 8208 | tf_op jit(solution)/shard_map/reduce_scatter | solution.py:352
  1199.4 138.8 %reduce-scatter.13.cloned.1.call-done = f32[128,128]{1,0:T(8,128)} async-done(((f32[4096,128]{1,0:T(8,128)}), f32[128,128]{1,0:T(8,128)}) %reduce-scatter.13.cloned.1.call-update) | async-done | bytes 65552 | tf_op jit(solution)/shard_map/reduce_scatter | solution.py:350
  1338.2 140.4 %reduce-scatter.11.cloned.1.call-done = f32[128,160]{0,1:T(8,128)} async-done(((f32[4096,160]{0,1:T(8,128)}), f32[128,160]{0,1:T(8,128)}) %reduce-scatter.11.cloned.1.call-update) | async-done | bytes 81936 | tf_op jit(solution)/shard_map/reduce_scatter | solution.py:349
  1478.7 710.9 %reduce-scatter.17.cloned.1.call-done = f32[128,2048]{1,0:T(8,128)} async-done(((f32[4096,2048]{1,0:T(8,128)}), f32[128,2048]{1,0:T(8,128)}) %reduce-scatter.17.cloned.1.call-update) | async-done | bytes 1048592 | tf_op jit(solution)/shard_map/reduce_scatter | solution.py:354
  2189.5 1405.5 %reduce-scatter.9.cloned.1.call-done = f32[64,8192]{1,0:T(8,128)} async-done(((f32[2048,8192]{1,0:T(8,128)}), f32[64,8192]{1,0:T(8,128)}) %reduce-scatter.9.cloned.1.call-update) | async-done | bytes 2097168 | tf_op jit(solution)/shard_map/reduce_scatter | solution.py:346
  (1218 shorter events, 352.4 us)
Async XLA Ops:
  7.2 199.9 %copy-start.6 = (bf16[1,128,2048]{2,1,0:T(8,128)(2,1)S(1)}, bf16[1,128,2048]{2,1,0:T(8,128)(2,1)}, u32[]{:S(2)}) copy-start(bf16[1,128,2048]{2,1,0:T(8,128)(2,1)} %param.22) | copy-start | bytes 1572868
  7.2 48.7 %copy-start.30 = (bf16[128,4]{0,1:T(4,128)(2,1)S(1)}, bf16[128,4]{0,1:T(4,128)(2,1)}, u32[]{:S(2)}) copy-start(bf16[128,4]{0,1:T(4,128)(2,1)} %param.25) | copy-start | bytes 3076
  7.2 112.5 %copy-start.29 = (bf16[128,16]{0,1:T(8,128)(2,1)S(1)}, bf16[128,16]{0,1:T(8,128)(2,1)}, u32[]{:S(2)}) copy-start(bf16[128,16]{0,1:T(8,128)(2,1)} %param.30) | copy-start | bytes 12292
  7.2 199.9 %all-gather.14.cloned.1.call-start = ((), (), s32[]{:S(2)}) async-start(), calls=%async_computation.6 | async-start | bytes 34603008 | tf_op jit(solution)/shard_map/all_gather | solution.py:184
  7.9 349.9 %all-gather.20.cloned.1.call-start = ((), (), s32[]{:S(2)}) async-start(), calls=%async_computation.9 | async-start | bytes 17301504 | tf_op jit(solution)/shard_map/all_gather | solution.py:192
  8.7 367.7 %all-gather.16.cloned.1.call-start = ((), (), s32[]{:S(2)}) async-start(), calls=%async_computation.7 | async-start | bytes 1351680 | tf_op jit(solution)/shard_map/all_gather | solution.py:187
  9.4 422.5 %all-gather.18.cloned.1.call-start = ((), (), s32[]{:S(2)}) async-start(), calls=%async_computation.8 | async-start | bytes 1081344 | tf_op jit(solution)/shard_map/all_gather | solution.py:188
  10.0 572.3 %all-gather.22.cloned.1.call-start = ((), (), s32[]{:S(2)}) async-start(), calls=%async_computation.15 | async-start | bytes 2359296 | tf_op jit(solution)/shard_map/all_gather | solution.py:24
  55.9 166.4 %copy-start.26 = (f32[128]{0:T(128)}, f32[128]{0:T(128)S(1)}, u32[]{:S(2)}) copy-start(f32[128]{0:T(128)S(1)} %add_rsqrt_fusion) | copy-start | bytes 1540
  189.2 38.6 %copy-start.31 = (bf16[128]{0:T(256)(128)(2,1)S(1)}, bf16[128]{0:T(256)(128)(2,1)}, u32[]{:S(2)}) copy-start(bf16[128]{0:T(256)(128)(2,1)} %param.26) | copy-start | bytes 772
  189.2 102.2 %copy-start.32 = (bf16[128]{0:T(256)(128)(2,1)S(1)}, bf16[128]{0:T(256)(128)(2,1)}, u32[]{:S(2)}) copy-start(bf16[128]{0:T(256)(128)(2,1)} %param.29) | copy-start | bytes 772
  222.3 5.4 copy-start.3
  222.3 133.9 %collective-permute-start = (bf16[3,4096]{1,0:T(4,128)(2,1)S(1)}, bf16[3,4096]{1,0:T(4,128)(2,1)S(1)}, u32[]{:S(2)}, u32[]{:S(2)}) collective-permute-start(bf16[3,4096]{1,0:T(4,128)(2,1)S(1)} %slice.804), channel_id=1, source_target_pairs={{0,1},{1,2},{2,3},{3,4},{4,5},{5,6},{6,7},{8,9},{9,10},{10,11},{11... | collective-permute-start | bytes 73736 | tf_op jit(solution)/shard_map/ppermute | solution.py:17
  227.7 130.2 %copy-start.18 = (f32[1,4096]{1,0:T(1,128)}, f32[1,4096]{1,0:T(1,128)S(1)}, u32[]{:S(2)}) copy-start(f32[1,4096]{1,0:T(1,128)S(1)} %get-tuple-element.971) | copy-start | bytes 49156
  227.7 130.2 %copy-start.20 = (f32[1,4096]{1,0:T(1,128)}, f32[1,4096]{1,0:T(1,128)S(1)}, u32[]{:S(2)}) copy-start(f32[1,4096]{1,0:T(1,128)S(1)} %get-tuple-element.972) | copy-start | bytes 49156
  227.7 130.2 %copy-start.22 = (f32[1,4096]{1,0:T(1,128)}, f32[1,4096]{1,0:T(1,128)S(1)}, u32[]{:S(2)}) copy-start(f32[1,4096]{1,0:T(1,128)S(1)} %get-tuple-element.973) | copy-start | bytes 49156
  227.7 130.2 %copy-start.24 = (f32[1,4096]{1,0:T(1,128)}, f32[1,4096]{1,0:T(1,128)S(1)}, u32[]{:S(2)}) copy-start(f32[1,4096]{1,0:T(1,128)S(1)} %get-tuple-element.974) | copy-start | bytes 49156
  227.7 128.5 %slice-start = ((bf16[128,8192]{1,0:T(8,128)(2,1)}), bf16[128,4096]{1,0:T(8,128)(2,1)S(1)}, s32[]{:S(2)}) async-start(bf16[128,8192]{1,0:T(8,128)(2,1)} %copy-done.3), calls=%async_computation.19 | async-start | bytes 2097152 | tf_op jit(solution)/shard_map/slice | solution.py:140
  356.2 1.7 copy-start.13
  433.6 3.1 copy-start.2
  443.1 139.2 %all-gather.24.cloned.1.call-start = ((), (), s32[]{:S(2)}) async-start(), calls=%async_computation.16 | async-start | bytes 2359296 | tf_op jit(solution)/shard_map/all_gather | solution.py:24
  444.8 74.3 %copy-start.33 = (bf16[128]{0:T(256)(128)(2,1)S(1)}, bf16[128]{0:T(256)(128)(2,1)}, u32[]{:S(2)}) copy-start(bf16[128]{0:T(256)(128)(2,1)} %param.31) | copy-start | bytes 772
  518.4 0.7 copy-start
  519.1 169.5 %all-gather.26.cloned.1.call-start = ((), (), s32[]{:S(2)}) async-start(), calls=%async_computation.17 | async-start | bytes 2359296 | tf_op jit(solution)/shard_map/all_gather | solution.py:24
  601.2 467.8 %reduce-scatter.19.cloned.1.call-start = ((), (), s32[]{:S(2)}) async-start(), calls=%async_computation.18 | async-start | bytes 2162688
  917.7 3.0 copy-start.11
  917.7 3.6 copy-start.12
  917.7 3.6 copy-start.17
  920.7 1.8 copy-start.16
  929.5 269.9 %reduce-scatter.15.cloned.1.call-start = ((), (), s32[]{:S(2)}) async-start(), calls=%async_computation.13 | async-start | bytes 270336 | tf_op jit(solution)/shard_map/reduce_scatter | solution.py:352
  930.4 407.9 %reduce-scatter.13.cloned.1.call-start = ((), (), s32[]{:S(2)}) async-start(), calls=%async_computation.12 | async-start | bytes 2162688 | tf_op jit(solution)/shard_map/reduce_scatter | solution.py:350
  932.3 546.4 %reduce-scatter.11.cloned.1.call-start = ((), (), s32[]{:S(2)}) async-start(), calls=%async_computation.11 | async-start | bytes 2703360 | tf_op jit(solution)/shard_map/reduce_scatter | solution.py:349
  934.3 1.6 copy-start.1
  934.4 1255.2 %reduce-scatter.17.cloned.1.call-start = ((), (), s32[]{:S(2)}) async-start(), calls=%async_computation.14 | async-start | bytes 34603008 | tf_op jit(solution)/shard_map/reduce_scatter | solution.py:354
  953.0 0.7 copy-start.19
  953.0 0.7 copy-start.21
  953.1 0.7 copy-start.23
  953.1 0.8 copy-start.25
  953.1 2641.9 %reduce-scatter.9.cloned.1.call-start = ((), (), s32[]{:S(2)}) async-start(), calls=%async_computation.10 | async-start | bytes 69206016 | tf_op jit(solution)/shard_map/reduce_scatter | solution.py:346
  953.8 8.9 copy-start.4
  953.8 8.9 copy-start.15
  958.5 6.8 collective-permute-start.1
  963.8 1.7 copy-start.9
  963.8 2.7 copy-start.7
  963.8 2.7 copy-start.27
  965.5 1.0 copy-start.10
  989.9 1.6 copy-start.5
  1002.2 18.9 copy-start.28
  1002.2 65.6 %copy-start.8 = (bf16[1,128,2048]{2,1,0:T(8,128)(2,1)S(1)}, bf16[1,128,2048]{2,1,0:T(8,128)(2,1)}, u32[]{:S(2)}) copy-start(bf16[1,128,2048]{2,1,0:T(8,128)(2,1)} %param.22) | copy-start | bytes 1572868
  1002.2 65.6 %copy-start.14 = (bf16[1,128,2048]{2,1,0:T(8,128)(2,1)S(1)}, bf16[1,128,2048]{2,1,0:T(8,128)(2,1)}, u32[]{:S(2)}) copy-start(bf16[1,128,2048]{2,1,0:T(8,128)(2,1)} %param.33) | copy-start | bytes 1572868
Sparse Core Ops, SparseCore 0:
  11.0 196.0 all-gather.13
  210.1 115.1 all-gather.19
  328.3 48.0 all-gather.15
  379.3 52.6 all-gather.17
  443.2 47.9 all-gather.21
  519.2 48.0 all-gather.23
  601.4 52.8 all-gather.25
  929.6 135.1 reduce-scatter.18
  1067.6 131.7 reduce-scatter.14
  1202.1 136.0 reduce-scatter.12
  1341.1 137.5 reduce-scatter.10
  1481.4 708.0 reduce-scatter.16
  2192.5 1402.4 reduce-scatter.8
where the time goes:
time: 3610 us; the launch traced here: 3600 us
  waiting for transfers between devices  2600 us (72%)
  blocking collectives  413 us (11%)
  other arithmetic  222 us (6%)
  local copies, waits for them, and re-layouts  219 us (6%)
  matrix products  113 us (3%)
    reduce_scatter x1, waiting for transfers between devices, shards(): lax.psum_scatter(grad_in_weight, ('dp', 'seq'), scatter_dimension=0, tile...  1410 us
    reduce_scatter x1, waiting for transfers between devices, shards(): lax.psum_scatter(grad_out_weight, ('dp', 'seq'), scatter_dimension=0, til...  711 us
    reduce_scatter x1, waiting for transfers between devices, shards(): lax.psum_scatter(grad_select, ('dp', 'seq'), scatter_dimension=0, tiled=T...  140 us
    reduce_scatter x1, waiting for transfers between devices, shards(): lax.psum_scatter(grad_step_weight, ('dp', 'seq'), scatter_dimension=0, ti...  139 us
    reduce_scatter x1, waiting for transfers between devices, shards(): lax.psum_scatter(grad_decay_log, ('dp', 'seq'), scatter_dimension=0, tile...  129 us
    slice x48, local copies, waits for them, and re-layouts, run_block(): inner_blk[position]  104 us
    unnamed x2, blocking collectives  88 us
  transfers between devices with their start and end apart: 15, of which 9 were waited for; matrix products, arithmetic and copies ran while one was open for 8% of the time, Pallas kernels for 0%

commit v1 on v0

v1 whole, which is shorter than its diff:
```python
import functools
import jax
import jax.numpy as jnp
from jax import lax
from jax.experimental import pallas as pl
from jax.experimental.pallas import tpu as pltpu
from jax.sharding import PartitionSpec as P

RANK = 128
KERNEL = 4
MESH = pl.DeviceIdType.MESH

CH = 8
NG = 8


def _expand(dst, pick_ref, base, first, chunk):
    cols = pick_ref.shape[0]
    width = NG * 128
    k_at = lax.broadcasted_iota(jnp.int32, (cols, width), 0)
    n_at = lax.broadcasted_iota(jnp.int32, (cols, width), 1) // 128
    pick_one = jnp.where(k_at == base + first + n_at, 1.0, 0.0).astype(jnp.bfloat16)
    for c in range(CH):
        tokens = pick_ref[:, c * chunk : (c + 1) * chunk]
        wide = lax.dot_general(
            tokens, pick_one, (((0,), (0,)), ((), ())), preferred_element_type=jnp.float32
        )
        for n in range(NG):
            dst.at[n][pl.ds(c, chunk, stride=CH), :] = wide[:, n * 128 : (n + 1) * 128]


def _weave(dst, value, chunk):
    for q in range(dst.shape[0]):
        for c in range(CH):
            dst.at[q][pl.ds(c, chunk, stride=CH), :] = value(
                slice(c * chunk, (c + 1) * chunk), slice(q * 128, (q + 1) * 128)
            )


def _unweave(dst, src, chunk):
    for q in range(src.shape[0]):
        for c in range(CH):
            dst[c * chunk : (c + 1) * chunk, q * 128 : (q + 1) * 128] = src.at[q][
                pl.ds(c, chunk, stride=CH), :
            ]


def _rows_mask(k, up):
    row = lax.broadcasted_iota(jnp.int32, (CH, 128), 0)
    return row < CH - k if up else row >= k


def _link(p, h, up):
    for k in (1, 2, 4):
        mask = _rows_mask(k, up)
        shift = CH - k if up else k
        ps = jnp.where(mask, pltpu.roll(p, shift, 0), 1.0)
        hs = jnp.where(mask, pltpu.roll(h, shift, 0), 0.0)
        h = h + p * hs
        p = p * ps
    return p, h


def fwd_kernel(chunk, lw, rank, state, delta_ref, inner_ref, pick_ref, a2_ref, h0_ref, y_ref, hin_ref, hend_ref, wx, rx, ab, dt, ut, yt):
    el = delta_ref.shape[1]
    _weave(dt, lambda i, j: delta_ref[i, j], chunk)
    _weave(ut, lambda i, j: delta_ref[i, j] * inner_ref[i, j], chunk)
    for g in range(state // NG):
        _expand(wx, pick_ref, rank, g * NG, chunk)
        _expand(rx, pick_ref, rank + state, g * NG, chunk)
        for q in range(el // (128 * lw)):
            tile = [q * lw + l for l in range(lw)]
            lanes = [slice((q * lw + l) * 128, (q * lw + l + 1) * 128) for l in range(lw)]
            rate = [[a2_ref[g * NG + n : g * NG + n + 1, lanes[l]] for l in range(lw)] for n in range(NG)]
            zero = jnp.zeros((CH, 128), jnp.float32)

            def first(t, carry):
                h, cum = carry
                row = pl.ds(pl.multiple_of(t * CH, CH), CH)
                d = [dt[tile[l], row, :] for l in range(lw)]
                du = [ut[tile[l], row, :] for l in range(lw)]
                out = []
                for n in range(NG):
                    w = wx[n, row, :]
                    for l in range(lw):
                        a = jnp.exp2(d[l] * rate[n][l])
                        ab[n * lw + l, row, :] = a
                        out.append(a * h[n * lw + l] + w * du[l])
                return tuple(out), tuple(cum[l] + d[l] for l in range(lw))

            h, cum = lax.fori_loop(
                0, chunk, first, ((zero,) * (NG * lw), (zero,) * lw), unroll=2
            )
            start = []
            for n in range(NG):
                for l in range(lw):
                    h0 = h0_ref[g * NG + n : g * NG + n + 1, lanes[l]]
                    p, hh = _link(jnp.exp2(cum[l] * rate[n][l]), h[n * lw + l], False)
                    full = hh + p * h0
                    begin = jnp.where(_rows_mask(1, False), pltpu.roll(full, 1, 0), h0)
                    hin_ref[g * NG + n, :, lanes[l]] = begin
                    hend_ref[g * NG + n : g * NG + n + 1, lanes[l]] = full[CH - 1 : CH]
                    start.append(begin)

            def second(t, h):
                row = pl.ds(pl.multiple_of(t * CH, CH), CH)
                du = [ut[tile[l], row, :] for l in range(lw)]
                out = []
                y = [None] * lw
                for n in range(NG):
                    w = wx[n, row, :]
                    r = rx[n, row, :]
                    for l in range(lw):
                        a = ab[n * lw + l, row, :]
                        hn = a * h[n * lw + l] + w * du[l]
                        out.append(hn)
                        y[l] = r * hn if n == 0 else y[l] + r * hn
                for l in range(lw):
                    yt[tile[l], row, :] = y[l] if g == 0 else yt[tile[l], row, :] + y[l]
                return tuple(out)

            lax.fori_loop(0, chunk, second, tuple(start), unroll=2)
    _unweave(y_ref, yt, chunk)


def scan_fwd(delta, inner, pick, a2, h0, rank, state):
    length, el = delta.shape
    chunk = length // CH
    lw = 2 if el % 256 == 0 else 1
    f32 = jnp.float32
    return pl.pallas_call(
        functools.partial(fwd_kernel, chunk, lw, rank, state),
        out_shape=(
            jax.ShapeDtypeStruct((length, el), f32),
            jax.ShapeDtypeStruct((state, CH, el), f32),
            jax.ShapeDtypeStruct((state, el), f32),
        ),
        in_specs=[pl.BlockSpec(memory_space=pltpu.VMEM)] * 5,
        out_specs=[pl.BlockSpec(memory_space=pltpu.VMEM)] * 3,
        scratch_shapes=[
            pltpu.VMEM((NG, length, 128), f32),
            pltpu.VMEM((NG, length, 128), f32),
            pltpu.VMEM((NG * lw, length, 128), f32),
        ]
        + [pltpu.VMEM((el // 128, length, 128), f32)] * 3,
        compiler_params=pltpu.CompilerParams(vmem_limit_bytes=60 << 20),
        name="scan_fwd",
    )(delta, inner, pick, a2, h0)


def bwd_kernel(chunk, lw, rank, state, delta_ref, inner_ref, gs_ref, pick_ref, a2_ref, hin_ref, k0_ref, s1_ref, s2_ref, gd_ref, gwr_ref, kend_ref, wx, rx, gw, gr, ab, hb, dt, ut, gt, s1t, s2t):
    el = delta_ref.shape[1]
    _weave(dt, lambda i, j: delta_ref[i, j], chunk)
    _weave(ut, lambda i, j: delta_ref[i, j] * inner_ref[i, j], chunk)
    _weave(gt, lambda i, j: gs_ref[i, j], chunk)
    for g in range(state // NG):
        _expand(wx, pick_ref, rank, g * NG, chunk)
        _expand(rx, pick_ref, rank + state, g * NG, chunk)
        for q in range(el // (128 * lw)):
            tile = [q * lw + l for l in range(lw)]
            lanes = [slice((q * lw + l) * 128, (q * lw + l + 1) * 128) for l in range(lw)]
            rate = [[a2_ref[g * NG + n : g * NG + n + 1, lanes[l]] for l in range(lw)] for n in range(NG)]
            zero = jnp.zeros((CH, 128), jnp.float32)
            begin = []
            for n in range(NG):
                for l in range(lw):
                    h = hin_ref[g * NG + n, :, lanes[l]]
                    hb[n * lw + l, 0:CH, :] = h
                    begin.append(h)

            def ahead(t, carry):
                h, cum = carry
                row = pl.ds(pl.multiple_of(t * CH, CH), CH)
                d = [dt[tile[l], row, :] for l in range(lw)]
                du = [ut[tile[l], row, :] for l in range(lw)]
                later = pl.ds(pl.multiple_of(t * CH + CH, CH), CH)
                out = []
                for n in range(NG):
                    w = wx[n, row, :]
                    for l in range(lw):
                        col = n * lw + l
                        a = jnp.exp2(d[l] * rate[n][l])
                        ab[col, row, :] = a
                        hn = a * h[n * lw + l] + w * du[l]
                        hb[col, later, :] = hn
                        out.append(hn)
                return tuple(out), tuple(cum[l] + d[l] for l in range(lw))

            unused, cum = lax.fori_loop(
                0, chunk, ahead, (tuple(begin), (zero,) * lw), unroll=2
            )

            def local(i, k):
                t = chunk - 1 - i
                row = pl.ds(pl.multiple_of(t * CH, CH), CH)
                gs = [gt[tile[l], row, :] for l in range(lw)]
                out = []
                for n in range(NG):
                    r = rx[n, row, :]
                    for l in range(lw):
                        col = n * lw + l
                        out.append(ab[col, row, :] * (k[n * lw + l] + r * gs[l]))
                return tuple(out)

            k = lax.fori_loop(0, chunk, local, (zero,) * (NG * lw), unroll=2)
            start = []
            for n in range(NG):
                for l in range(lw):
                    k0 = k0_ref[g * NG + n : g * NG + n + 1, lanes[l]]
                    p, kk = _link(jnp.exp2(cum[l] * rate[n][l]), k[n * lw + l], True)
                    full = kk + p * k0
                    start.append(jnp.where(_rows_mask(1, True), pltpu.roll(full, CH - 1, 0), k0))
                    kend_ref[g * NG + n : g * NG + n + 1, lanes[l]] = full[0:1]

            def final(i, carry):
                k, gd = carry
                t = chunk - 1 - i
                row = pl.ds(pl.multiple_of(t * CH, CH), CH)
                d = [dt[tile[l], row, :] for l in range(lw)]
                du = [ut[tile[l], row, :] for l in range(lw)]
                gs = [gt[tile[l], row, :] for l in range(lw)]
                later = pl.ds(pl.multiple_of(t * CH + CH, CH), CH)
                ko, gdo = [], []
                s1 = [None] * lw
                s2 = [None] * lw
                for n in range(NG):
                    w = wx[n, row, :]
                    r = rx[n, row, :]
                    gwn = grn = None
                    for l in range(lw):
                        col = n * lw + l
                        gh = k[n * lw + l] + r * gs[l]
                        kn = ab[col, row, :] * gh
                        q_ = kn * hb[col, row, :]
                        ko.append(kn)
                        gdo.append(gd[n * lw + l] + q_ * d[l])
                        f1 = rate[n][l] * q_
                        f2 = gh * w
                        s1[l] = f1 if n == 0 else s1[l] + f1
                        s2[l] = f2 if n == 0 else s2[l] + f2
                        gwn = gh * du[l] if l == 0 else gwn + gh * du[l]
                        hr = gs[l] * hb[col, later, :]
                        grn = hr if l == 0 else grn + hr
                    gw[n, row, :] = gwn if q == 0 else gw[n, row, :] + gwn
                    gr[n, row, :] = grn if q == 0 else gr[n, row, :] + grn
                for l in range(lw):
                    s1t[tile[l], row, :] = s1[l] if g == 0 else s1t[tile[l], row, :] + s1[l]
                    s2t[tile[l], row, :] = s2[l] if g == 0 else s2t[tile[l], row, :] + s2[l]
                return tuple(ko), tuple(gdo)

            unused, gd = lax.fori_loop(
                0, chunk, final, (tuple(start), (zero,) * (NG * lw)), unroll=1
            )
            for n in range(NG):
                for l in range(lw):
                    gd_ref[g * NG + n : g * NG + n + 1, lanes[l]] = jnp.sum(gd[n * lw + l], axis=0, keepdims=True)

        c_at = lax.broadcasted_iota(jnp.int32, (2 * state, 128), 0)
        for c in range(CH):
            rows = pl.ds(c, chunk, stride=CH)
            here = slice(c * chunk, (c + 1) * chunk)
            part = None if g == 0 else gwr_ref[:, here]
            for n in range(NG):
                for src, base in ((gw, 0), (gr, state)):
                    ones = jnp.where(c_at == base + g * NG + n, 1.0, 0.0).astype(jnp.bfloat16)
                    one = lax.dot_general(
                        ones,
                        src.at[n][rows, :].astype(jnp.bfloat16),
                        (((1,), (1,)), ((), ())),
                        preferred_element_type=jnp.float32,
                    )
                    part = one if part is None else part + one
            gwr_ref[:, here] = part
    _unweave(s1_ref, s1t, chunk)
    _unweave(s2_ref, s2t, chunk)


def scan_bwd(delta, inner, gs, pick, a2, hin, k0, rank, state):
    length, el = delta.shape
    chunk = length // CH
    lw = 2 if el % 256 == 0 else 1
    f32 = jnp.float32
    return pl.pallas_call(
        functools.partial(bwd_kernel, chunk, lw, rank, state),
        out_shape=(
            jax.ShapeDtypeStruct((length, el), f32),
            jax.ShapeDtypeStruct((length, el), f32),
            jax.ShapeDtypeStruct((state, el), f32),
            jax.ShapeDtypeStruct((2 * state, length), f32),
            jax.ShapeDtypeStruct((state, el), f32),
        ),
        in_specs=[pl.BlockSpec(memory_space=pltpu.VMEM)] * 7,
        out_specs=[pl.BlockSpec(memory_space=pltpu.VMEM)] * 5,
        scratch_shapes=[pltpu.VMEM((NG, length, 128), f32)] * 4
        + [
            pltpu.VMEM((NG * lw, length, 128), f32),
            pltpu.VMEM((NG * lw, length + CH, 128), f32),
        ]
        + [pltpu.VMEM((el // 128, length, 128), f32)] * 5,
        compiler_params=pltpu.CompilerParams(vmem_limit_bytes=63 << 20),
        name="scan_bwd",
    )(delta, inner, gs, pick, a2, hin, k0)


EPS = 1e-05
LN2 = 0.6931471805599453
SEGMENT = 1024
BF = jnp.bfloat16
F32 = jnp.float32


def peers_barrier(seq_peers, dp_peers):
    barrier = pltpu.get_barrier_semaphore()
    for p in seq_peers:
        pl.semaphore_signal(barrier, inc=1, device_id={"seq": p}, device_id_type=MESH)
    for p in dp_peers:
        pl.semaphore_signal(barrier, inc=1, device_id={"dp": p}, device_id_type=MESH)
    pl.semaphore_wait(barrier, len(seq_peers) + len(dp_peers))


def sum_kernel(n, part_ref, out_ref, recv, send_sem, recv_sem, back_send, back_recv):
    me = lax.axis_index("seq")
    peers = [lax.rem(me + k, n) for k in range(1, n)]
    peers_barrier(peers, [])

    def at(p):
        return pl.ds(pl.multiple_of(p * 128, 128), 128)

    out = [
        pltpu.make_async_remote_copy(
            src_ref=part_ref.at[:, at(p)],
            dst_ref=recv.at[k],
            send_sem=send_sem.at[k],
            recv_sem=recv_sem.at[k],
            device_id={"seq": p},
            device_id_type=MESH,
        )
        for k, p in enumerate(peers)
    ]
    for c in out:
        c.start()
    total = part_ref[:, at(me)].astype(F32)
    for k, c in enumerate(out):
        c.wait_recv()
        total = total + recv[k].astype(F32)
    out_ref[:, at(me)] = total.astype(BF)
    back = [
        pltpu.make_async_remote_copy(
            src_ref=out_ref.at[:, at(me)],
            dst_ref=out_ref.at[:, at(me)],
            send_sem=back_send.at[k],
            recv_sem=back_recv.at[k],
            device_id={"seq": p},
            device_id_type=MESH,
        )
        for k, p in enumerate(peers)
    ]
    for c in back:
        c.start()
    for c in out:
        c.wait_send()
    for c in back:
        c.wait()


def sum_over_seq(part, n, name, ident):
    rows, length = part.shape
    return pl.pallas_call(
        functools.partial(sum_kernel, n),
        out_shape=jax.ShapeDtypeStruct((rows, length), BF),
        in_specs=[pl.BlockSpec(memory_space=pltpu.VMEM)],
        out_specs=pl.BlockSpec(memory_space=pltpu.VMEM),
        scratch_shapes=[pltpu.VMEM((n - 1, rows, 128), BF)] + [pltpu.SemaphoreType.DMA((n - 1,))] * 4,
        compiler_params=pltpu.CompilerParams(collective_id=ident, has_side_effects=True),
        name=name,
    )(part)


SLAB = 32


def front_kernel(xn, wp, pk, xg, wg, pg, local_sem, z_send, z_recv, y_send, y_recv, w_send, w_recv, d_send, d_recv, p_send, p_recv):
    s = lax.axis_index("seq")
    d = lax.axis_index("dp")
    n = 8
    z, y = s // 2, lax.rem(s, 2)
    other = s + 1 - 2 * y
    cross = lax.rem(d + 2, 4)
    core = d + 1 - 2 * lax.rem(d, 2)
    peers = [lax.rem(s + k, n) for k in range(1, n)]
    peers_barrier(peers, [cross, core])
    col = xn.shape[0] // SLAB

    def slab(c):
        return pl.ds(c * SLAB, SLAB)

    own = [
        pltpu.make_async_copy(xn, xg.at[s], local_sem.at[0]),
        pltpu.make_async_copy(wp.at[s], wg.at[d, s], local_sem.at[1]),
        pltpu.make_async_copy(pk, pg.at[d], local_sem.at[2]),
    ]

    def copy(src, dst, ss, rs, to):
        return pltpu.make_async_remote_copy(
            src_ref=src, dst_ref=dst, send_sem=ss, recv_sem=rs, device_id=to, device_id_type=MESH
        )

    chains = [(c, y) for c in range(col)] + [(col - 1, 1 - y)]

    def z_copy(chain, up, j):
        c, yy = chains[chain]
        block = (z - j if up else z + j) * 2 + yy
        src = xn.at[slab(c)] if (j == 0 and chain < col) else xg.at[block, slab(c)]
        at = chain * 6 + (0 if up else 3) + j
        return copy(src, xg.at[block, slab(c)], z_send.at[at], z_recv.at[at], {"seq": s + 2 if up else s - 2})

    def z_arrived(chain, up, j):
        c, yy = chains[chain]
        block = (z - j if up else z + j) * 2 + yy
        at = chain * 6 + (0 if up else 3) + j - 1
        ref = xg.at[block, slab(c)]
        return copy(ref, ref, z_send.at[at], z_recv.at[at], {"seq": s})

    def can(up, j):
        return z >= j if up else z <= 3 - j

    def can_send(up):
        return z < 3 if up else z > 0

    def y_copy(chain, where):
        c = chains[chain][0]
        block = (z + where) * 2 + y
        src = xn.at[slab(c)] if where == 0 else xg.at[block, slab(c)]
        at = chain * 7 + where + 3
        return copy(src, xg.at[block, slab(c)], y_send.at[at], y_recv.at[at], {"seq": other})

    def w_copy(k):
        return copy(wp.at[peers[k]], wg.at[d, s], w_send.at[k], w_recv.at[k], {"seq": peers[k]})

    def w_from(k):
        source = lax.rem(s + n - 1 - k, n)
        ref = wg.at[d, source]
        return copy(ref, ref, w_send.at[k], w_recv.at[k], {"seq": s}), source

    def d_copy(k, source, kind):
        block = cross if kind == 2 else d
        src = wp.at[s] if (k == 7 and kind < 2) else wg.at[block, source]
        at = k * 3 + kind
        return copy(src, wg.at[block, source], d_send.at[at], d_recv.at[at], {"dp": cross if kind == 0 else core})

    def d_from(k, source, kind):
        block = cross if kind == 0 else (core if kind == 1 else 3 - d)
        return block

    def p_copy(c, kind):
        block = cross if kind == 2 else d
        rows = slab(c)
        src = pk.at[rows] if kind < 2 else pg.at[block, rows]
        at = c * 3 + kind
        return copy(src, pg.at[block, rows], p_send.at[at], p_recv.at[at], {"dp": cross if kind == 0 else core})

    for k in range(n - 1):
        w_copy(k).start()
    y_copy(col - 1, 0).start()
    for chain in range(col):
        for up in (True, False):

            @pl.when(can_send(up))
            def _():
                z_copy(chain, up, 0).start()

        if chain < col - 1:
            y_copy(chain, 0).start()
    for kind in (0, 1):
        d_copy(7, s, kind).start()
    for c in range(col):
        for kind in (0, 1):
            p_copy(c, kind).start()
    for c in own:
        c.start()

    sources = []
    for k in range(n - 1):
        sources.append(lax.rem(s + n - 1 - k, n))
    sources.append(s)

    def w_relay(k):
        arrived, source = w_from(k)
        arrived.wait_recv()
        for kind in (0, 1):
            d_copy(k, source, kind).start()

    def cross_relay(k):
        source = sources[k]
        ref = wg.at[cross, source]
        copy(ref, ref, d_send.at[k * 3], d_recv.at[k * 3], {"seq": s}).wait_recv()
        d_copy(k, source, 2).start()

    def z_round(j):
        for chain in range(col + 1):
            for up in (True, False):

                @pl.when(can(up, j))
                def _():
                    z_arrived(chain, up, j).wait_recv()
                    if j < 3:

                        @pl.when(can_send(up))
                        def _():
                            z_copy(chain, up, j).start()

                    if chain < col - 1:
                        y_copy(chain, -j if up else j).start()

    def y_arrived(chain, where):
        c = chains[chain][0]
        ref = xg.at[(z + where) * 2 + 1 - y, slab(c)]
        at = chain * 7 + where + 3
        return copy(ref, ref, y_send.at[at], y_recv.at[at], {"seq": s})

    y_arrived(col - 1, 0).wait_recv()
    for up in (True, False):

        @pl.when(can_send(up))
        def _():
            z_copy(col, up, 0).start()

    z_round(1)
    for k in (0, 1, 5, 6):
        w_relay(k)
    z_round(2)
    for k in (2, 3, 4):
        w_relay(k)
    for c in range(col):
        ref = pg.at[cross, slab(c)]
        copy(ref, ref, p_send.at[c * 3], p_recv.at[c * 3], {"seq": s}).wait_recv()
        p_copy(c, 2).start()
    z_round(3)
    for k in (7, 0, 1, 5, 6, 2, 3, 4):
        cross_relay(k)
    for chain in range(col - 1):
        y_arrived(chain, 0).wait_recv()
        for j in (1, 2, 3):
            for up in (True, False):

                @pl.when(can(up, j))
                def _():
                    y_arrived(chain, -j if up else j).wait_recv()

    diag = lax.rem(core + 2, 4)
    for k in range(n):
        for kind, block in ((1, core), (2, diag)):
            ref = wg.at[block, sources[k]]
            at = k * 3 + kind
            copy(ref, ref, d_send.at[at], d_recv.at[at], {"seq": s}).wait_recv()
    for c in range(col):
        for kind, block in ((1, core), (2, diag)):
            ref = pg.at[block, slab(c)]
            at = c * 3 + kind
            copy(ref, ref, p_send.at[at], p_recv.at[at], {"seq": s}).wait_recv()
    for k in range(n - 1):
        w_copy(k).wait_send()
    for k in range(n):
        for kind in (0, 1, 2):
            d_copy(k, sources[k], kind).wait_send()
    for c in range(col):
        for kind in (0, 1, 2):
            p_copy(c, kind).wait_send()
    y_copy(col - 1, 0).wait_send()
    for chain in range(col - 1):
        y_copy(chain, 0).wait_send()
        for j in (1, 2, 3):
            for up in (True, False):

                @pl.when(can(up, j))
                def _():
                    y_copy(chain, -j if up else j).wait_send()

    for chain in range(col + 1):
        for up in (True, False):

            @pl.when(can_send(up))
            def _():
                z_copy(chain, up, 0).wait_send()

            for j in (1, 2):

                @pl.when(jnp.logical_and(can(up, j), can_send(up)))
                def _():
                    z_copy(chain, up, j).wait_send()

    for c in own:
        c.wait()


def front_gather(xn, wp, pk):
    col = xn.shape[0] // SLAB
    dma = pltpu.SemaphoreType.DMA
    return pl.pallas_call(
        front_kernel,
        out_shape=(
            jax.ShapeDtypeStruct((8,) + xn.shape, BF),
            jax.ShapeDtypeStruct((4,) + wp.shape, BF),
            jax.ShapeDtypeStruct((4,) + pk.shape, BF),
        ),
        in_specs=[pl.BlockSpec(memory_space=pltpu.VMEM)] * 3,
        out_specs=[pl.BlockSpec(memory_space=pltpu.VMEM)] * 3,
        scratch_shapes=[
            dma((3,)),
            dma(((col + 1) * 6,)),
            dma(((col + 1) * 6,)),
            dma((col * 7,)),
            dma((col * 7,)),
            dma((7,)),
            dma((7,)),
            dma((24,)),
            dma((24,)),
            dma((col * 3,)),
            dma((col * 3,)),
        ],
        compiler_params=pltpu.CompilerParams(
            collective_id=3, has_side_effects=True, vmem_limit_bytes=40 << 20
        ),
        name="front_gather",
    )(xn, wp, pk)


def silu_slope(values_in):
    sigmoid_value = jax.nn.sigmoid(values_in)
    return sigmoid_value * (1.0 + values_in * (1.0 - sigmoid_value))


def dot(a, b, dims):
    return lax.dot_general(a, b, (dims, ((), ())), preferred_element_type=F32)


def segments(length):
    count = max(1, length // SEGMENT)
    size = length // count
    return [(i * size, (i + 1) * size) for i in range(count)]


def forward_scan(step_size, inner, picked, rate2):
    state = rate2.shape[0]
    carry = jnp.zeros(rate2.shape, F32)
    outs, starts = [], []
    for lo, hi in segments(step_size.shape[0]):
        y, start, carry = scan_fwd(step_size[lo:hi], inner[lo:hi], picked[:, lo:hi], rate2, carry, RANK, state)
        outs.append(y)
        starts.append(start)
    return (outs[0] if len(outs) == 1 else jnp.concatenate(outs, axis=0)), starts


def backward_scan(step_size, inner, grad_scan, picked, rate2, starts):
    state = rate2.shape[0]
    carry = jnp.zeros(rate2.shape, F32)
    parts = []
    total = jnp.zeros(rate2.shape, F32)
    spans = segments(step_size.shape[0])
    for (lo, hi), start in reversed(list(zip(spans, starts))):
        s1, s2, decay, gwr, carry = scan_bwd(
            step_size[lo:hi], inner[lo:hi], grad_scan[lo:hi], picked[:, lo:hi], rate2, start, carry, RANK, state
        )
        total = total + decay
        parts.append((s1, s2, gwr))
    parts = parts[::-1]
    if len(parts) == 1:
        s1, s2, gwr = parts[0]
    else:
        s1, s2, gwr = (jnp.concatenate(p, axis=k) for k, p in zip((0, 0, 1), zip(*parts)))
    return s1, s2, gwr, total


def shards(
    block_input,
    norm_gain,
    in_weight,
    conv_weight,
    conv_bias,
    select_weight,
    step_weight,
    step_bias,
    decay_log,
    skip_gain,
    out_weight,
    output_grad,
):
    n_dp, n_seq = lax.axis_size("dp"), lax.axis_size("seq")
    token_rows = block_input[0]
    upstream_rows = output_grad[0]
    width = token_rows.shape[1]
    d_rows = in_weight.shape[0]
    e_rows = out_weight.shape[0]
    local = n_dp * e_rows

    own = token_rows.astype(F32)
    own_scale = lax.rsqrt(jnp.mean(own * own, axis=1, keepdims=True) + EPS)
    own_normed = (own * own_scale).astype(BF)
    gain = norm_gain.astype(F32)[:, None]
    pieces = (in_weight.astype(F32) * gain).astype(BF)
    pieces = pieces.reshape(d_rows, 2, n_dp, n_seq, e_rows).transpose(3, 0, 1, 2, 4).reshape(n_seq, d_rows, 2 * local)

    smalls = [select_weight, step_weight, decay_log, conv_weight, conv_bias[:, None], step_bias[:, None], skip_gain[:, None]]
    used = sum(s.shape[1] for s in smalls)
    pad = -used % 128
    packed = jnp.concatenate([out_weight] + smalls + [jnp.zeros((e_rows, pad), BF)], axis=1)
    if (n_dp, n_seq) == (4, 8):
        normed, in_w, packed = front_gather(own_normed, pieces, packed)
        packed = packed.reshape(local, packed.shape[2])
    else:
        normed = lax.all_gather(own_normed, "seq")
        in_w = lax.all_gather(lax.all_to_all(pieces, "seq", 0, 0), "dp")
        packed = lax.all_gather(packed, "dp", axis=0, tiled=True)
    length = n_seq * token_rows.shape[0]
    normed = normed.reshape(length, width)
    in_w = in_w.reshape(width, 2 * local)
    upstream_rows, normed = lax.optimization_barrier((upstream_rows, normed))
    cuts = []
    begin = 0
    for s in [out_weight] + smalls:
        cuts.append((begin, begin + s.shape[1]))
        begin += s.shape[1]
    out_w, sel_w, step_w, dec_w, conv_w, conv_b, step_b, skip = (packed[:, a:b] for a, b in cuts)
    conv_taps = conv_w.astype(F32).T
    conv_b, step_b, skip = (v[:, 0].astype(F32) for v in (conv_b, step_b, skip))
    decay_rate = -jnp.exp(dec_w.astype(F32).T)
    rate2 = decay_rate * (1.0 / LN2)

    mixed = dot(normed, in_w, ((1,), (0,))).astype(BF)
    padded = jnp.concatenate([jnp.zeros((KERNEL - 1, local), BF), mixed[:, :local]], axis=0).astype(F32)
    gate_in = mixed[:, local:].astype(F32)
    conv_out = conv_b + jnp.zeros((length, local), F32)
    for offset in range(KERNEL):
        conv_out = conv_out + padded[offset : offset + length] * conv_taps[offset]
    inner = jax.nn.silu(conv_out).astype(BF)
    inner_f = inner.astype(F32)
    picked = sum_over_seq(dot(sel_w, inner, ((0,), (1,))).astype(BF), n_seq, "sum_picked", 1)
    step_in = picked[:RANK]
    step_raw = dot(step_in, step_w, ((0,), (1,))) + step_b
    step_size = jax.nn.softplus(step_raw)
    scanned, starts = forward_scan(step_size, inner_f, picked, rate2)
    mamba_out = scanned + skip * inner_f
    gate_act = jax.nn.silu(gate_in)
    gated_out = (mamba_out * gate_act).astype(BF)
    out_part = dot(gated_out, out_w, ((1,), (0,))).astype(BF)

    upstream = lax.all_gather(upstream_rows, "seq", axis=0, tiled=True)
    grad_gated = dot(upstream, out_w, ((1,), (1,)))
    grad_out_w = dot(gated_out, upstream, ((0,), (0,)))
    grad_scan = grad_gated * gate_act
    grad_gate = grad_gated * mamba_out * silu_slope(gate_in)
    grad_skip = jnp.sum(grad_scan * inner_f, axis=0)
    grad_scan, out_part = lax.optimization_barrier((grad_scan, out_part))
    s1, s2, grad_wr, grad_decay = backward_scan(step_size, inner_f, grad_scan, picked, rate2, starts)
    out_rows = lax.psum_scatter(out_part, "seq", scatter_dimension=0, tiled=True)
    layer_out = (token_rows.astype(F32) + out_rows.astype(F32)).astype(BF)
    grad_raw_f = (s1 * LN2 + inner_f * s2) * jax.nn.sigmoid(step_raw)
    grad_step_b = jnp.sum(grad_raw_f, axis=0)
    grad_raw = grad_raw_f.astype(BF)
    grad_step_w = dot(grad_raw, step_in, ((0,), (1,)))
    part = jnp.concatenate([dot(step_w, grad_raw, ((0,), (1,))), grad_wr], axis=0).astype(BF)
    grad_picked = sum_over_seq(part, n_seq, "sum_grad_picked", 2)
    grad_sel = dot(inner, grad_picked, ((0,), (1,)))
    grad_inner = step_size * s2 + grad_scan * skip + dot(grad_picked, sel_w, ((0,), (1,)))
    grad_conv = grad_inner * silu_slope(conv_out)
    grad_conv_b = jnp.sum(grad_conv, axis=0)
    grad_taps = [jnp.sum(grad_conv * padded[k : k + length], axis=0) for k in range(KERNEL)]
    extended = jnp.concatenate([grad_conv, jnp.zeros((KERNEL - 1, local), F32)], axis=0)
    grad_conv_in = jnp.zeros((length, local), F32)
    for k in range(KERNEL):
        grad_conv_in = grad_conv_in + extended[KERNEL - 1 - k : KERNEL - 1 - k + length] * conv_taps[k]
    grad_mixed = jnp.concatenate([grad_conv_in, grad_gate], axis=1).astype(BF)
    grad_in_w = dot(normed, grad_mixed, ((0,), (0,)))
    grad_normed = dot(grad_mixed, in_w, ((1,), (1,)))

    small_grads = [grad_sel, grad_step_w, (grad_decay * decay_rate).T, jnp.stack(grad_taps, axis=1), grad_conv_b[:, None], grad_step_b[:, None], grad_skip[:, None]]
    packed_grad = jnp.concatenate([grad_out_w] + small_grads + [jnp.zeros((local, pad), F32)], axis=1).astype(BF)
    packed_grad = lax.psum_scatter(packed_grad, "dp", scatter_dimension=0, tiled=True).astype(F32)
    g_out, g_sel, g_step, g_dec, g_conv, g_cb, g_sb, g_skip = (packed_grad[:, a:b] for a, b in cuts)

    grad_in_all = lax.psum_scatter(grad_in_w.astype(BF), "dp", scatter_dimension=0, tiled=True)
    grad_in_all = lax.all_to_all(grad_in_all, "seq", split_axis=0, concat_axis=0, tiled=True)
    grad_in_all = grad_in_all.reshape(n_seq, d_rows, 2, n_dp, e_rows).transpose(1, 2, 3, 0, 4).reshape(in_weight.shape).astype(F32)
    g_gain = jnp.sum(grad_in_all * in_weight.astype(F32), axis=1)
    g_in = grad_in_all * gain

    grad_normed = lax.psum_scatter(grad_normed.astype(BF), "seq", scatter_dimension=0, tiled=True).astype(F32)
    scaled = grad_normed
    grad_rows = own_scale * scaled - own * (own_scale * own_scale * own_scale) * jnp.mean(scaled * own, axis=1, keepdims=True)
    input_grad = (upstream_rows.astype(F32) + grad_rows).astype(BF)
    return (
        layer_out[None],
        input_grad[None],
        g_gain,
        g_in,
        g_conv,
        g_cb[:, 0],
        g_sel,
        g_step,
        g_sb[:, 0],
        g_dec,
        g_skip[:, 0],
        g_out,
    )


def solution(mesh):
    rows = P(("dp", "seq"))
    both = P(("dp", "seq"), None)
    acts = P("dp", "seq", None)
    return jax.shard_map(
        shards,
        mesh=mesh,
        in_specs=(acts, rows, both, both, rows, both, both, rows, both, rows, both, acts),
        out_specs=(acts, acts, rows, both, both, rows, both, both, rows, both, rows, both),
        check_vma=False,
    )
```

time: 3610 us -> 629 us (0.17)
  waiting for transfers between devices: 2600 us -> 273 us
  blocking collectives: 413 us -> 0 us
  Pallas kernels: 0 us -> 195 us
  other arithmetic: 222 us -> 30.1 us
  local copies, waits for them, and re-layouts: 219 us -> 43.6 us
  matrix products: 113 us -> 57.3 us
    reduce_scatter x5 -> x4, waiting for transfers between devices: 2520 us -> 220 us  [the longest x1 90.2 us: shards(): lax.psum_scatter(out_part, 'seq', scatter_dimension=0, tiled=True)]
    all_gather x5 -> x0, blocking collectives: 325 us -> none  [the longest x1 69.4 us: shards(): lax.all_gather(decay_log, ('dp', 'seq'), axis=0, tiled=True)]
    pallas_call x0 -> x5, Pallas kernels: none -> 195 us  [the longest x1 67.7 us: front_gather(): pl.pallas_call(front_kernel, out_shape=(jax.ShapeDtypeStruct((8,) + xn.sh...]
    reduce_sum x179 -> x4, other arithmetic: 142 us -> 8.58 us  [the longest x1 4.09 us: shards(): grad_step_b = jnp.sum(grad_raw_f, axis=0)]
    slice x70 -> x9, local copies, waits for them, and re-layouts: 132 us -> 8.79 us  [the longest x6 7.09 us: shards(): packed_grad[:, a:b]]
    unnamed x2 -> x0, blocking collectives: 88 us -> none
    dot_general x12, matrix products: 113 us -> 57.3 us  [dot(): return lax.dot_general(a, b, (dims, ((), ())), preferred_element_type=F32)]
    add x24 -> x0, other arithmetic: 41.8 us -> none  [the longest x16 29 us: retreat(): grad_decay + block_grads[5]]
  transfers between devices with their start and end apart: 15 -> 6, of which waited for: 9 -> 5; matrix products, arithmetic and copies ran while one was open for 8% -> 9% of each run, Pallas kernels for 0% -> 0%
where the time goes in v1:
time: 629 us; the launch traced here: 621 us
  waiting for transfers between devices  273 us (43%)
  Pallas kernels  195 us (31%)
  matrix products  57.3 us (9%)
  local copies, waits for them, and re-layouts  43.6 us (7%)
  other arithmetic  30.1 us (5%)
  between operations  14.8 us (2%)
  starting transfers between devices  6.48 us (1%)
    reduce_scatter x1, waiting for transfers between devices, shards(): lax.psum_scatter(out_part, 'seq', scatter_dimension=0, tiled=True)  90.2 us
    reduce_scatter x1, waiting for transfers between devices, shards(): lax.psum_scatter(grad_normed.astype(BF), 'seq', scatter_dimension=0, tile...  82.8 us
    pallas_call x1, Pallas kernels, front_gather(): pl.pallas_call(front_kernel, out_shape=(jax.ShapeDtypeStruct((8,) + xn.sh...  67.7 us
    dot_general x12, matrix products, dot(): return lax.dot_general(a, b, (dims, ((), ())), preferred_element_type=F32)  57.3 us
    pallas_call x1, Pallas kernels, scan_bwd(): pl.pallas_call(functools.partial(bwd_kernel, chunk, lw, rank, state), out...  57.1 us
    all_gather x1, waiting for transfers between devices, shards(): upstream = lax.all_gather(upstream_rows, 'seq', axis=0, tiled=True)  52.5 us
    pallas_call x2, Pallas kernels, sum_over_seq(): pl.pallas_call(functools.partial(sum_kernel, n), out_shape=jax.ShapeDtype...  41.4 us
    reduce_scatter x1, waiting for transfers between devices, shards(): lax.psum_scatter(packed_grad, 'dp', scatter_dimension=0, tiled=True)  30.2 us
  transfers between devices with their start and end apart: 6, of which 5 were waited for; matrix products, arithmetic and copies ran while one was open for 9% of the time, Pallas kernels for 0%

profile of v1, /device:TPU:12, one launch (start us, length us, event | category | flops | bytes accessed | tf_op | source)
XLA Modules:
  0.0 621.2 jit_solution(10209779277946329841)
XLA Ops:
  8.0 1.2 fusion.16
  9.7 0.8 copy.64
  10.5 0.8 copy.65
  11.3 0.8 copy.66
  12.1 0.8 copy.63
  12.9 0.8 copy.67
  13.7 0.9 copy.62
  14.6 1.2 fusion.17.xn
  16.8 0.8 reshape.91.wp
  18.0 67.7 %front_gather.1 = (bf16[8,128,2048]{2,1,0:T(8,128)(2,1)S(1)}, bf16[4,8,64,1024]{3,2,1,0:T(8,128)(2,1)S(1)}, bf16[4,128,2432]{2,1,0:T(8,128)(2,1)S(1)}) custom-call(bf16[128,2048]{1,0:T(8,128)(2,1)S(1)} %fusion.17.xn, bf16[8,64,1024]{2,1,0:T(8,128)(2,1)S(1)} %reshape.91.wp, bf16[128,2432]{1,0:T(8,128)(2,1)S(1)} %concatenate.21.pk), custom_call_target="tpu_custom_call" | custom-call | tf_op jit(solution)/shard_map/front_gather/pallas_call | solution.py:599
  85.7 1.4 copy-done
  87.1 1.9 copy-done.2
  89.1 1.9 copy-done.3
  91.1 1.0 slice.144
  92.2 1.0 slice_convert_fusion.2
  93.3 1.4 slice_convert_fusion
  96.7 8.5 %convolution_convert_fusion.4 = bf16[1024,1024]{1,0:T(8,128)(2,1)S(1)} fusion(bf16[1024,2048]{1,0:T(8,128)(2,1)} %bitcast.74, bf16[2048,1024]{1,0:T(8,128)(2,1)} %bitcast.72), kind=kOutput, calls=%fused_computation.41 | convolution fusion | flops 4296015872 | bytes 10485760 | tf_op jit(solution)/shard_map/dot_general | solution.py:634
  105.2 1.3 copy-done.14
  107.8 1.6 pad_convert_fusion
  109.5 52.5 %all-gather.2.cloned.1.call-done = bf16[1024,2048]{1,0:T(8,128)(2,1)} async-done(((bf16[128,2048]{1,0:T(8,128)(2,1)}), bf16[1024,2048]{1,0:T(8,128)(2,1)}) %all-gather.2.cloned.1.call-update) | async-done | bytes 4194320 | tf_op jit(solution)/shard_map/all_gather | solution.py:747
  162.0 11.0 %multiply_reduce_fusion = (bf16[512]{0:T(512)(128)(2,1)}, bf16[1024,512]{1,0:T(8,128)(2,1)S(1)}, f32[1024,512]{1,0:T(8,128)}, f32[1024,512]{1,0:T(8,128)}, f32[1024,512]{1,0:T(8,128)}) fusion(f32[512]{0:T(512)} %bitcast.89, f32[1027,512]{1,0:T(8,128)} %pad_convert_fusion, f32[512]{0:T(512)} %bitcast.91, f32[512]{0:T(512)} %bitcast.93, f32[512]{0:T(512)} %bitcast.87, ...), kind=kOutput, calls=%fused_computation.26 | convolution fusion | flops 2159017472 | bytes 23079936 | tf_op jit(solution)/shard_map/dot_general | solution.py:634
  173.0 1.2 convolution_convert_fusion.5.part_ref
  174.2 1.6 convert_element_type.135.inner_ref
  175.8 19.3 %sum_picked.1.pick_ref = bf16[160,1024]{1,0:T(8,128)(2,1)} custom-call(bf16[160,1024]{1,0:T(8,128)(2,1)} %convolution_convert_fusion.5.part_ref), custom_call_target="tpu_custom_call" | custom-call | tf_op jit(solution)/shard_map/sum_picked/pallas_call | solution.py:368
  195.2 4.3 compare_select_fusion
  200.1 29.3 %scan_fwd.1 = (f32[1024,512]{1,0:T(8,128)}, f32[16,8,512]{2,1,0:T(8,128)}, f32[16,512]{1,0:T(8,128)}) custom-call(f32[1024,512]{1,0:T(8,128)} %get-tuple-element.105.delta_ref, f32[1024,512]{1,0:T(8,128)} %convert_element_type.135.inner_ref, bf16[160,1024]{1,0:T(8,128)(2,1)} %sum_picked.1.pick_ref, f32[16,512]{1,0:T(8,128)} %bitcast_multiply_fusion.2.a2_ref, ...), custom_call_target="tpu_custom_call" | custom-call | tf_op jit(solution)/shard_map/scan_fwd/pallas_call | solution.py:131
  229.3 4.6 fusion.8
  233.9 1.0 copy-done.19
  234.9 4.3 convolution_convert_fusion
  239.2 57.1 %scan_bwd.1 = (f32[1024,512]{1,0:T(8,128)}, f32[1024,512]{1,0:T(8,128)}, f32[16,512]{1,0:T(8,128)}, f32[32,1024]{1,0:T(8,128)}, f32[16,512]{1,0:T(8,128)}) custom-call(f32[1024,512]{1,0:T(8,128)} %get-tuple-element.105.delta_ref, f32[1024,512]{1,0:T(8,128)} %convert_element_type.135.inner_ref, f32[1024,512]{1,0:T(8,128)} %get-tuple-element.32.gs_ref, ...), custom_call_target="tpu_custom_call" | custom-call | tf_op jit(solution)/shard_map/scan_bwd/pallas_call | solution.py:283
  296.3 0.9 convert.64
  297.3 4.1 fusion.39
  301.4 1.7 convolution_convert_fusion.6
  303.8 22.1 %sum_grad_picked.1 = bf16[160,1024]{1,0:T(8,128)(2,1)} custom-call(bf16[160,1024]{1,0:T(8,128)(2,1)} %pad_maximum_fusion.3.part_ref), custom_call_target="tpu_custom_call" | custom-call | tf_op jit(solution)/shard_map/sum_grad_picked/pallas_call | solution.py:368
  326.0 4.2 multiply_multiply_fusion
  330.3 2.0 multiply_reduce_fusion.1
  332.3 1.0 copy-done.20
  333.3 6.4 %convolution_convert_fusion.1 = bf16[2048,1024]{1,0:T(8,128)(2,1)} fusion(bf16[1024,2048]{1,0:T(8,128)(2,1)S(1)} %bitcast.75, bf16[1024,512]{1,0:T(8,128)(2,1)S(1)} %copy-done.17, bf16[1024,512]{1,0:T(8,128)(2,1)S(1)} %get-tuple-element.93), kind=kOutput, calls=%fused_computation.2 | convolution fusion | flops 4301258752 | bytes 10485760 | tf_op jit(solution)/shard_map/dot_general | solution.py:634
  341.2 0.8 broadcast_in_dim.53
  342.4 0.8 stack.23
  343.2 0.8 stack.22
  344.0 0.8 stack.21
  344.8 0.8 stack.20
  345.6 0.8 broadcast_in_dim.52
  346.4 1.1 convolution_convert_fusion.8
  347.6 5.3 convolution_convert_fusion.3
  353.0 4.9 concatenate.26
  358.0 1.1 copy-done.18
  359.5 9.0 %convolution_convert_fusion.2 = bf16[1024,2048]{1,0:T(8,128)(2,1)} fusion(bf16[2048,1024]{1,0:T(8,128)(2,1)} %bitcast.73, bf16[1024,512]{1,0:T(8,128)(2,1)S(1)} %copy-done.18, bf16[1024,512]{1,0:T(8,128)(2,1)S(1)} %copy-done.21), kind=kOutput, calls=%fused_computation.3 | convolution fusion | flops 4301258752 | bytes 10485760 | tf_op jit(solution)/shard_map/dot_general | solution.py:634
  369.1 17.0 %reduce-scatter.9.cloned.1.call-done = bf16[512,1024]{1,0:T(8,128)(2,1)} async-done(((bf16[2048,1024]{1,0:T(8,128)(2,1)}), bf16[512,1024]{1,0:T(8,128)(2,1)}) %reduce-scatter.9.cloned.1.call-update) | async-done | bytes 1048592 | tf_op jit(solution)/shard_map/reduce_scatter | solution.py:781
  386.1 6.0 all-to-all-start
  392.2 30.2 %reduce-scatter.11.cloned.1.call-done = bf16[128,2432]{1,0:T(8,128)(2,1)} async-done(((bf16[512,2432]{1,0:T(8,128)(2,1)}), bf16[128,2432]{1,0:T(8,128)(2,1)}) %reduce-scatter.11.cloned.1.call-update) | async-done | bytes 622608 | tf_op jit(solution)/shard_map/reduce_scatter | solution.py:778
  422.4 0.9 slice.151
  423.9 0.8 slice.146
  425.4 0.8 slice.148
  427.0 1.5 slice.149
  428.6 2.2 slice.153
  431.6 82.8 %reduce-scatter.7.cloned.1.call-done = bf16[128,2048]{1,0:T(8,128)(2,1)} async-done(((bf16[1024,2048]{1,0:T(8,128)(2,1)}), bf16[128,2048]{1,0:T(8,128)(2,1)}) %reduce-scatter.7.cloned.1.call-update) | async-done | bytes 524304 | tf_op jit(solution)/shard_map/reduce_scatter | solution.py:787
  514.4 1.3 fusion.20
  515.7 90.2 %reduce-scatter.5.cloned.1.call-done = bf16[128,2048]{1,0:T(8,128)(2,1)} async-done(((bf16[1024,2048]{1,0:T(8,128)(2,1)}), bf16[128,2048]{1,0:T(8,128)(2,1)}) %reduce-scatter.5.cloned.1.call-update) | async-done | bytes 524304 | tf_op jit(solution)/shard_map/reduce_scatter | solution.py:755
  605.9 2.6 fusion.24
  608.5 0.9 reshape.100
  609.5 1.2 copy.69
  610.7 3.5 bitcast_multiply_fusion
  (123 shorter events, 13.6 us)
Async XLA Ops:
  7.2 8.6 %copy-start.11 = (bf16[64,8192]{1,0:T(8,128)(2,1)S(1)}, bf16[64,8192]{1,0:T(8,128)(2,1)}, u32[]{:S(2)}) copy-start(bf16[64,8192]{1,0:T(8,128)(2,1)} %param.14) | copy-start | bytes 3145732
  7.2 154.8 %all-gather.2.cloned.1.call-start = ((), (), s32[]{:S(2)}) async-start(), calls=%async_computation.5 | async-start | bytes 4718592 | tf_op jit(solution)/shard_map/all_gather | solution.py:747
  8.0 8.4 %copy-start.39 = (f32[64]{0:T(128)}, f32[64]{0:T(128)S(1)}, u32[]{:S(2)}) copy-start(f32[64]{0:T(128)S(1)} %convert_element_type.124) | copy-start | bytes 772
  9.7 6.6 %copy-start.41 = (f32[128]{0:T(128)}, f32[128]{0:T(128)S(1)}, u32[]{:S(2)}) copy-start(f32[128]{0:T(128)S(1)} %get-tuple-element.103) | copy-start | bytes 1540
  16.4 1.2 copy-start.29
  16.4 1.2 copy-start.30
  85.7 1.5 copy-start
  87.1 1.9 copy-start.2
  89.1 1.9 copy-start.3
  91.0 295.1 %reduce-scatter.9.cloned.1.call-start = ((), (), s32[]{:S(2)}) async-start(), calls=%async_computation.8 | async-start | bytes 5242880 | tf_op jit(solution)/shard_map/reduce_scatter | solution.py:781
  105.2 1.3 copy-start.14
  106.6 55.4 %copy-start.1 = (bf16[4,128,2432]{2,1,0:T(8,128)(2,1)S(1)}, bf16[4,128,2432]{2,1,0:T(8,128)(2,1)}, u32[]{:S(2)}) copy-start(bf16[4,128,2432]{2,1,0:T(8,128)(2,1)} %copy-done) | copy-start | bytes 7471108
  173.0 56.3 %copy-start.6 = (bf16[1024,512]{1,0:T(8,128)(2,1)}, bf16[1024,512]{1,0:T(8,128)(2,1)S(1)}, u32[]{:S(2)}) copy-start(bf16[1024,512]{1,0:T(8,128)(2,1)S(1)} %get-tuple-element.83) | copy-start | bytes 3145732
  200.0 29.3 %copy-start.32 = (f32[512,1]{0,1:T(1,128)S(1)}, f32[512,1]{0,1:T(1,128)}, u32[]{:S(2)}) copy-start(f32[512,1]{0,1:T(1,128)} %copy.98) | copy-start | bytes 6148
  233.9 1.0 copy-start.19
  239.2 58.0 %copy-start.34 = (f32[512,1]{0,1:T(1,128)S(1)}, f32[512,1]{0,1:T(1,128)}, u32[]{:S(2)}) copy-start(f32[512,1]{0,1:T(1,128)} %copy.97) | copy-start | bytes 6148
  301.3 24.6 %copy-start.8 = (f32[1024,512]{1,0:T(8,128)S(1)}, f32[1024,512]{1,0:T(8,128)}, u32[]{:S(2)}) copy-start(f32[1024,512]{1,0:T(8,128)} %get-tuple-element.105.delta_ref) | copy-start | bytes 6291460
  301.3 24.6 %copy-start.33 = (f32[512,1]{0,1:T(1,128)S(1)}, f32[512,1]{0,1:T(1,128)}, u32[]{:S(2)}) copy-start(f32[512,1]{0,1:T(1,128)} %copy.98) | copy-start | bytes 6148
  325.9 4.3 copy-start.5
  325.9 4.3 copy-start.35
  325.9 4.3 copy-start.36
  326.0 4.3 copy-start.37
  326.0 4.3 copy-start.38
  330.3 3.0 copy-start.4
  330.3 3.0 copy-start.17
  332.3 1.0 copy-start.20
  339.6 0.6 copy-start.43
  339.6 0.8 copy-start.31
  339.6 2.3 copy-start.7
  339.6 2.3 copy-start.16
  339.7 6.7 %copy-start.13 = (bf16[160,1024]{1,0:T(8,128)(2,1)S(1)}, bf16[160,1024]{1,0:T(8,128)(2,1)}, u32[]{:S(2)}) copy-start(bf16[160,1024]{1,0:T(8,128)(2,1)} %sum_picked.1.pick_ref) | copy-start | bytes 983044
  339.7 82.7 %reduce-scatter.11.cloned.1.call-start = ((), (), s32[]{:S(2)}) async-start(), calls=%async_computation.9 | async-start | bytes 3112960 | tf_op jit(solution)/shard_map/reduce_scatter | solution.py:778
  347.5 5.4 copy-start.22
  347.5 5.4 copy-start.23
  347.5 5.4 copy-start.24
  347.5 5.4 copy-start.25
  347.5 5.4 copy-start.26
  347.6 5.4 copy-start.27
  347.6 5.4 copy-start.28
  357.9 1.2 copy-start.18
  357.9 1.5 copy-start.21
  358.0 156.4 %reduce-scatter.7.cloned.1.call-start = ((), (), s32[]{:S(2)}) async-start(), calls=%async_computation.7 | async-start | bytes 4718592 | tf_op jit(solution)/shard_map/reduce_scatter | solution.py:787
  368.5 237.3 %reduce-scatter.5.cloned.1.call-start = ((), (), s32[]{:S(2)}) async-start(), calls=%async_computation.6 | async-start | bytes 4718592 | tf_op jit(solution)/shard_map/reduce_scatter | solution.py:755
  386.1 222.3 %all-to-all-start = ((bf16[8,64,1024]{2,1,0:T(8,128)(2,1)}), bf16[8,64,1024]{2,1,0:T(8,128)(2,1)S(1)}, u32[]{:S(2)}, u32[]{:S(2)}) async-start(bf16[8,64,1024]{2,1,0:T(8,128)(2,1)} %bitcast.81), calls=%async_computation.3 | async-start | bytes 2097152 | tf_op jit(solution)/shard_map/all_to_all | solution.py:782
  422.4 8.4 %copy-start.10 = (bf16[128,2432]{1,0:T(8,128)(2,1)S(1)}, bf16[128,2432]{1,0:T(8,128)(2,1)}, u32[]{:S(2)}) copy-start(bf16[128,2432]{1,0:T(8,128)(2,1)} %reduce-scatter.11.cloned.1.call-done) | copy-start | bytes 1867780
  428.6 85.8 %copy-start.9 = (bf16[1,128,2048]{2,1,0:T(8,128)(2,1)S(1)}, bf16[1,128,2048]{2,1,0:T(8,128)(2,1)}, u32[]{:S(2)}) copy-start(bf16[1,128,2048]{2,1,0:T(8,128)(2,1)} %param.12) | copy-start | bytes 1572868
  428.6 177.3 %copy-start.15 = (bf16[1,128,2048]{2,1,0:T(8,128)(2,1)S(1)}, bf16[1,128,2048]{2,1,0:T(8,128)(2,1)}, u32[]{:S(2)}) copy-start(bf16[1,128,2048]{2,1,0:T(8,128)(2,1)} %param.23) | copy-start | bytes 1572868
  428.6 177.3 %copy-start.42 = (f32[128]{0:T(128)S(1)}, f32[128]{0:T(128)}, u32[]{:S(2)}) copy-start(f32[128]{0:T(128)} %copy-done.41) | copy-start | bytes 1540
  428.6 177.3 %copy-start.44 = (f32[128]{0:T(128)S(1)}, f32[128]{0:T(128)}, u32[]{:S(2)}) copy-start(f32[128]{0:T(128)} %get-tuple-element.102) | copy-start | bytes 1540
  609.4 1.2 copy-start.12
  609.4 1.2 copy-start.40
Sparse Core Ops, SparseCore 0:
  91.2 70.8 all-gather.1
  339.8 46.2 reduce-scatter.8
  388.7 33.6 reduce-scatter.10
  425.8 88.5 reduce-scatter.6
  517.9 87.9 reduce-scatter.4

commit v2 on v1

v2 whole, which is shorter than its diff:
```python
import functools
import jax
import jax.numpy as jnp
from jax import lax
from jax.experimental import pallas as pl
from jax.experimental.pallas import tpu as pltpu
from jax.sharding import PartitionSpec as P

RANK = 128
KERNEL = 4
MESH = pl.DeviceIdType.MESH
HIDE = True
BF = jnp.bfloat16
F32 = jnp.float32

CH = 8


def _expand(dst, pick_ref, base, first, chunk):
    ng = dst.shape[0]
    cols = pick_ref.shape[0]
    width = ng * 128
    k_at = lax.broadcasted_iota(jnp.int32, (cols, width), 0)
    n_at = lax.broadcasted_iota(jnp.int32, (cols, width), 1) // 128
    pick_one = jnp.where(k_at == base + first + n_at, 1.0, 0.0).astype(BF)
    for c in range(CH):
        tokens = pick_ref[:, c * chunk : (c + 1) * chunk]
        wide = lax.dot_general(
            tokens, pick_one, (((0,), (0,)), ((), ())), preferred_element_type=F32
        )
        for n in range(ng):
            dst.at[n][pl.ds(c, chunk, stride=CH), :] = wide[:, n * 128 : (n + 1) * 128]


def _weave(dst, value, chunk):
    for q in range(dst.shape[0]):
        for c in range(CH):
            dst.at[q][pl.ds(c, chunk, stride=CH), :] = value(
                slice(c * chunk, (c + 1) * chunk), slice(q * 128, (q + 1) * 128)
            )


def _unweave(dst, src, chunk):
    for q in range(src.shape[0]):
        for c in range(CH):
            dst[c * chunk : (c + 1) * chunk, q * 128 : (q + 1) * 128] = src.at[q][
                pl.ds(c, chunk, stride=CH), :
            ]


def _rows_mask(k, up):
    row = lax.broadcasted_iota(jnp.int32, (CH, 128), 0)
    return row < CH - k if up else row >= k


def _link(p, h, up):
    for k in (1, 2, 4):
        mask = _rows_mask(k, up)
        shift = CH - k if up else k
        ps = jnp.where(mask, pltpu.roll(p, shift, 0), 1.0)
        hs = jnp.where(mask, pltpu.roll(h, shift, 0), 0.0)
        h = h + p * hs
        p = p * ps
    return p, h


def _split_loop(total, parts, body, carry, unroll, point):
    size = total // parts
    for i in range(parts):
        carry = lax.fori_loop(i * size, (i + 1) * size, body, carry, unroll=unroll)
        point()
    return carry


def fwd_kernel(chunk, lw, ng, rank, state, hide, *refs):
    delta_ref, inner_ref, pick_ref, a2_ref, h0_ref = refs[:5]
    refs = refs[5:]
    extra_in, refs = refs[:hide], refs[hide:]
    y_ref, hin_ref, hend_ref = refs[:3]
    refs = refs[3:]
    extra_out, refs = refs[:hide], refs[hide:]
    wx, rx, ab, dt, ut, yt = refs[:6]
    todo = []
    if hide:
        sems = refs[6:10]
        local_sem = refs[10]
        s = lax.axis_index("seq")
        d = lax.axis_index("dp")
        peers_barrier([lax.rem(s + k, 8) for k in range(1, 8)], [lax.rem(d + 2, 4), d + 1 - 2 * lax.rem(d, 2)])
        start, steps, finish = gather_stages(extra_in[0], extra_out[0], *sems)
        start()
        own = pltpu.make_async_copy(extra_in[0], extra_out[0].at[s], local_sem)
        own.start()
        skip = lambda: None
        todo = [steps[0], skip, steps[1], skip, steps[2], skip, steps[3], skip]

    def point():
        if todo:
            todo.pop(0)()

    el = delta_ref.shape[1]
    _weave(dt, lambda i, j: delta_ref[i, j], chunk)
    _weave(ut, lambda i, j: delta_ref[i, j] * inner_ref[i, j], chunk)
    for g in range(state // ng):
        _expand(wx, pick_ref, rank, g * ng, chunk)
        _expand(rx, pick_ref, rank + state, g * ng, chunk)
        for q in range(el // (128 * lw)):
            tile = [q * lw + l for l in range(lw)]
            lanes = [slice((q * lw + l) * 128, (q * lw + l + 1) * 128) for l in range(lw)]
            rate = [[a2_ref[g * ng + n : g * ng + n + 1, lanes[l]] for l in range(lw)] for n in range(ng)]
            zero = jnp.zeros((CH, 128), F32)

            def first(t, carry):
                h, cum = carry
                row = pl.ds(pl.multiple_of(t * CH, CH), CH)
                d = [dt[tile[l], row, :] for l in range(lw)]
                du = [ut[tile[l], row, :] for l in range(lw)]
                out = []
                for n in range(ng):
                    w = wx[n, row, :]
                    for l in range(lw):
                        a = jnp.exp2(d[l] * rate[n][l])
                        ab[n * lw + l, row, :] = a
                        out.append(a * h[n * lw + l] + w * du[l])
                return tuple(out), tuple(cum[l] + d[l] for l in range(lw))

            h, cum = _split_loop(chunk, 1, first, ((zero,) * (ng * lw), (zero,) * lw), 4, point)
            begin_at = []
            for n in range(ng):
                for l in range(lw):
                    h0 = h0_ref[g * ng + n : g * ng + n + 1, lanes[l]]
                    p, hh = _link(jnp.exp2(cum[l] * rate[n][l]), h[n * lw + l], False)
                    full = hh + p * h0
                    begin = jnp.where(_rows_mask(1, False), pltpu.roll(full, 1, 0), h0)
                    hin_ref[g * ng + n, :, lanes[l]] = begin
                    hend_ref[g * ng + n : g * ng + n + 1, lanes[l]] = full[CH - 1 : CH]
                    begin_at.append(begin)

            def second(t, h):
                row = pl.ds(pl.multiple_of(t * CH, CH), CH)
                du = [ut[tile[l], row, :] for l in range(lw)]
                out = []
                y = [None] * lw
                for n in range(ng):
                    w = wx[n, row, :]
                    r = rx[n, row, :]
                    for l in range(lw):
                        a = ab[n * lw + l, row, :]
                        hn = a * h[n * lw + l] + w * du[l]
                        out.append(hn)
                        y[l] = r * hn if n == 0 else y[l] + r * hn
                for l in range(lw):
                    yt[tile[l], row, :] = y[l] if g == 0 else yt[tile[l], row, :] + y[l]
                return tuple(out)

            _split_loop(chunk, 1, second, tuple(begin_at), 4, point)
    while todo:
        point()
    _unweave(y_ref, yt, chunk)
    if hide:
        finish()
        own.wait()


def scan_fwd(delta, inner, pick, a2, h0, rank, state, shard=None):
    length, el = delta.shape
    chunk = length // CH
    lw = min(4, el // 128)
    ng = 4 if lw == 4 else 8
    f32 = F32
    vmem = pl.BlockSpec(memory_space=pltpu.VMEM)
    out_shape = [
        jax.ShapeDtypeStruct((length, el), f32),
        jax.ShapeDtypeStruct((state, CH, el), f32),
        jax.ShapeDtypeStruct((state, el), f32),
    ]
    out_specs = [vmem] * 3
    scratch = [
        pltpu.VMEM((ng, length, 128), f32),
        pltpu.VMEM((ng, length, 128), f32),
        pltpu.VMEM((ng * lw, length, 128), f32),
    ] + [pltpu.VMEM((el // 128, length, 128), f32)] * 3
    args = [delta, inner, pick, a2, h0]
    params = dict(vmem_limit_bytes=60 << 20)
    if shard is not None:
        args.append(shard)
        out_shape.append(jax.ShapeDtypeStruct((8,) + shard.shape, BF))
        out_specs.append(pl.BlockSpec(memory_space=pl.ANY))
        scratch += gather_sems(shard.shape[0]) + [pltpu.SemaphoreType.DMA]
        params.update(collective_id=5, has_side_effects=True)
    return pl.pallas_call(
        functools.partial(fwd_kernel, chunk, lw, ng, rank, state, 0 if shard is None else 1),
        out_shape=tuple(out_shape),
        in_specs=[vmem] * len(args),
        out_specs=tuple(out_specs),
        scratch_shapes=scratch,
        compiler_params=pltpu.CompilerParams(**params),
        name="scan_fwd",
    )(*args)


def bwd_kernel(chunk, lw, ng, rank, state, hide, *refs):
    delta_ref, inner_ref, gs_ref, pick_ref, a2_ref, hin_ref, k0_ref = refs[:7]
    refs = refs[7:]
    extra_in, refs = refs[:hide], refs[hide:]
    s1_ref, s2_ref, gd_ref, gwr_ref, kend_ref = refs[:5]
    refs = refs[5:]
    extra_out, refs = refs[:hide], refs[hide:]
    wx, rx, gw, gr, ab, hb, dt, ut, gt, s1t, s2t = refs[:11]
    todo = []
    if hide:
        s = lax.axis_index("seq")
        d = lax.axis_index("dp")
        peers_barrier([lax.rem(s + k, 8) for k in range(1, 8)], [lax.rem(d + 2, 4), d + 1 - 2 * lax.rem(d, 2)])
        start, todo, finish = scatter_stages(extra_in[0], extra_out[0], *refs[11:21])
        todo = list(todo)
        start()

    def point():
        if todo:
            todo.pop(0)()

    el = delta_ref.shape[1]
    _weave(dt, lambda i, j: delta_ref[i, j], chunk)
    _weave(ut, lambda i, j: delta_ref[i, j] * inner_ref[i, j], chunk)
    _weave(gt, lambda i, j: gs_ref[i, j], chunk)
    for g in range(state // ng):
        _expand(wx, pick_ref, rank, g * ng, chunk)
        _expand(rx, pick_ref, rank + state, g * ng, chunk)
        for q in range(el // (128 * lw)):
            tile = [q * lw + l for l in range(lw)]
            lanes = [slice((q * lw + l) * 128, (q * lw + l + 1) * 128) for l in range(lw)]
            rate = [[a2_ref[g * ng + n : g * ng + n + 1, lanes[l]] for l in range(lw)] for n in range(ng)]
            zero = jnp.zeros((CH, 128), F32)
            begin = []
            for n in range(ng):
                for l in range(lw):
                    h = hin_ref[g * ng + n, :, lanes[l]]
                    hb[n * lw + l, 0:CH, :] = h
                    begin.append(h)

            def ahead(t, carry):
                h, cum = carry
                row = pl.ds(pl.multiple_of(t * CH, CH), CH)
                d = [dt[tile[l], row, :] for l in range(lw)]
                du = [ut[tile[l], row, :] for l in range(lw)]
                later = pl.ds(pl.multiple_of(t * CH + CH, CH), CH)
                out = []
                for n in range(ng):
                    w = wx[n, row, :]
                    for l in range(lw):
                        col = n * lw + l
                        a = jnp.exp2(d[l] * rate[n][l])
                        ab[col, row, :] = a
                        hn = a * h[n * lw + l] + w * du[l]
                        hb[col, later, :] = hn
                        out.append(hn)
                return tuple(out), tuple(cum[l] + d[l] for l in range(lw))

            unused, cum = _split_loop(chunk, 1, ahead, (tuple(begin), (zero,) * lw), 4, point)

            def local(i, k):
                t = chunk - 1 - i
                row = pl.ds(pl.multiple_of(t * CH, CH), CH)
                gs = [gt[tile[l], row, :] for l in range(lw)]
                out = []
                for n in range(ng):
                    r = rx[n, row, :]
                    for l in range(lw):
                        col = n * lw + l
                        out.append(ab[col, row, :] * (k[n * lw + l] + r * gs[l]))
                return tuple(out)

            k = _split_loop(chunk, 1, local, (zero,) * (ng * lw), 4, point)
            begin_at = []
            for n in range(ng):
                for l in range(lw):
                    k0 = k0_ref[g * ng + n : g * ng + n + 1, lanes[l]]
                    p, kk = _link(jnp.exp2(cum[l] * rate[n][l]), k[n * lw + l], True)
                    full = kk + p * k0
                    begin_at.append(jnp.where(_rows_mask(1, True), pltpu.roll(full, CH - 1, 0), k0))
                    kend_ref[g * ng + n : g * ng + n + 1, lanes[l]] = full[0:1]

            def final(i, carry):
                k, gd = carry
                t = chunk - 1 - i
                row = pl.ds(pl.multiple_of(t * CH, CH), CH)
                d = [dt[tile[l], row, :] for l in range(lw)]
                du = [ut[tile[l], row, :] for l in range(lw)]
                gs = [gt[tile[l], row, :] for l in range(lw)]
                later = pl.ds(pl.multiple_of(t * CH + CH, CH), CH)
                ko, gdo = [], []
                s1 = [None] * lw
                s2 = [None] * lw
                for n in range(ng):
                    w = wx[n, row, :]
                    r = rx[n, row, :]
                    gwn = grn = None
                    for l in range(lw):
                        col = n * lw + l
                        gh = k[n * lw + l] + r * gs[l]
                        kn = ab[col, row, :] * gh
                        q_ = kn * hb[col, row, :]
                        ko.append(kn)
                        gdo.append(gd[n * lw + l] + q_ * d[l])
                        f1 = rate[n][l] * q_
                        f2 = gh * w
                        s1[l] = f1 if n == 0 else s1[l] + f1
                        s2[l] = f2 if n == 0 else s2[l] + f2
                        gwn = gh * du[l] if l == 0 else gwn + gh * du[l]
                        hr = gs[l] * hb[col, later, :]
                        grn = hr if l == 0 else grn + hr
                    gw[n, row, :] = gwn if q == 0 else gw[n, row, :] + gwn
                    gr[n, row, :] = grn if q == 0 else gr[n, row, :] + grn
                for l in range(lw):
                    s1t[tile[l], row, :] = s1[l] if g == 0 else s1t[tile[l], row, :] + s1[l]
                    s2t[tile[l], row, :] = s2[l] if g == 0 else s2t[tile[l], row, :] + s2[l]
                return tuple(ko), tuple(gdo)

            unused, gd = _split_loop(chunk, 2, final, (tuple(begin_at), (zero,) * (ng * lw)), 2, point)
            for n in range(ng):
                for l in range(lw):
                    gd_ref[g * ng + n : g * ng + n + 1, lanes[l]] = jnp.sum(gd[n * lw + l], axis=0, keepdims=True)

        c_at = lax.broadcasted_iota(jnp.int32, (2 * state, 128), 0)
        for c in range(CH):
            rows = pl.ds(c, chunk, stride=CH)
            here = slice(c * chunk, (c + 1) * chunk)
            part = None if g == 0 else gwr_ref[:, here]
            for n in range(ng):
                for src, base in ((gw, 0), (gr, state)):
                    ones = jnp.where(c_at == base + g * ng + n, 1.0, 0.0).astype(BF)
                    one = lax.dot_general(
                        ones,
                        src.at[n][rows, :].astype(BF),
                        (((1,), (1,)), ((), ())),
                        preferred_element_type=F32,
                    )
                    part = one if part is None else part + one
            gwr_ref[:, here] = part
    while todo:
        point()
    _unweave(s1_ref, s1t, chunk)
    _unweave(s2_ref, s2t, chunk)
    if hide:
        finish()


def scan_bwd(delta, inner, gs, pick, a2, hin, k0, rank, state, part=None):
    length, el = delta.shape
    chunk = length // CH
    lw = min(4, el // 128)
    ng = 4 if lw == 4 else 8
    f32 = F32
    vmem = pl.BlockSpec(memory_space=pltpu.VMEM)
    out_shape = [
        jax.ShapeDtypeStruct((length, el), f32),
        jax.ShapeDtypeStruct((length, el), f32),
        jax.ShapeDtypeStruct((state, el), f32),
        jax.ShapeDtypeStruct((2 * state, length), f32),
        jax.ShapeDtypeStruct((state, el), f32),
    ]
    scratch = (
        [pltpu.VMEM((ng, length, 128), f32)] * 4
        + [pltpu.VMEM((ng * lw, length, 128), f32), pltpu.VMEM((ng * lw, length + CH, 128), f32)]
        + [pltpu.VMEM((el // 128, length, 128), f32)] * 5
    )
    args = [delta, inner, gs, pick, a2, hin, k0]
    params = dict(vmem_limit_bytes=67043328)
    if part is not None:
        args.append(part)
        out_shape.append(jax.ShapeDtypeStruct((part.shape[0] // 8, part.shape[1]), f32))
        scratch += scatter_scratch(part.shape[0] // 8, part.shape[1], 2)
        params.update(collective_id=6, has_side_effects=True)
    return pl.pallas_call(
        functools.partial(bwd_kernel, chunk, lw, ng, rank, state, 0 if part is None else 1),
        out_shape=tuple(out_shape),
        in_specs=[vmem] * len(args),
        out_specs=tuple([vmem] * len(out_shape)),
        scratch_shapes=scratch,
        compiler_params=pltpu.CompilerParams(**params),
        name="scan_bwd",
    )(*args)


EPS = 1e-05
LN2 = 0.6931471805599453
SEGMENT = 1024


def peers_barrier(seq_peers, dp_peers):
    barrier = pltpu.get_barrier_semaphore()
    for p in seq_peers:
        pl.semaphore_signal(barrier, inc=1, device_id={"seq": p}, device_id_type=MESH)
    for p in dp_peers:
        pl.semaphore_signal(barrier, inc=1, device_id={"dp": p}, device_id_type=MESH)
    pl.semaphore_wait(barrier, len(seq_peers) + len(dp_peers))


def sum_kernel(n, part_ref, out_ref, recv, send_sem, recv_sem, back_send, back_recv):
    me = lax.axis_index("seq")
    peers = [lax.rem(me + k, n) for k in range(1, n)]
    peers_barrier(peers, [])

    def at(p):
        return pl.ds(pl.multiple_of(p * 128, 128), 128)

    out = [
        pltpu.make_async_remote_copy(
            src_ref=part_ref.at[:, at(p)],
            dst_ref=recv.at[k],
            send_sem=send_sem.at[k],
            recv_sem=recv_sem.at[k],
            device_id={"seq": p},
            device_id_type=MESH,
        )
        for k, p in enumerate(peers)
    ]
    for c in out:
        c.start()
    total = part_ref[:, at(me)].astype(F32)
    for k, c in enumerate(out):
        c.wait_recv()
        total = total + recv[k].astype(F32)
    out_ref[:, at(me)] = total.astype(BF)
    back = [
        pltpu.make_async_remote_copy(
            src_ref=out_ref.at[:, at(me)],
            dst_ref=out_ref.at[:, at(me)],
            send_sem=back_send.at[k],
            recv_sem=back_recv.at[k],
            device_id={"seq": p},
            device_id_type=MESH,
        )
        for k, p in enumerate(peers)
    ]
    for c in back:
        c.start()
    for c in out:
        c.wait_send()
    for c in back:
        c.wait()


def sum_over_seq(part, n, name, ident):
    rows, length = part.shape
    return pl.pallas_call(
        functools.partial(sum_kernel, n),
        out_shape=jax.ShapeDtypeStruct((rows, length), BF),
        in_specs=[pl.BlockSpec(memory_space=pltpu.VMEM)],
        out_specs=pl.BlockSpec(memory_space=pltpu.VMEM),
        scratch_shapes=[pltpu.VMEM((n - 1, rows, 128), BF)] + [pltpu.SemaphoreType.DMA((n - 1,))] * 4,
        compiler_params=pltpu.CompilerParams(collective_id=ident, has_side_effects=True),
        name=name,
    )(part)


SLAB = 32


def remote(src, dst, ss, rs, to):
    return pltpu.make_async_remote_copy(
        src_ref=src, dst_ref=dst, send_sem=ss, recv_sem=rs, device_id=to, device_id_type=MESH
    )


def gather_stages(xn, xg, z_send, z_recv, y_send, y_recv):
    s = lax.axis_index("seq")
    z, y = s // 2, lax.rem(s, 2)
    other = s + 1 - 2 * y
    col = xn.shape[0] // SLAB
    chains = [(c, y) for c in range(col)] + [(col - 1, 1 - y)]

    def slab(c):
        return pl.ds(c * SLAB, SLAB)

    def z_copy(chain, up, j):
        c, yy = chains[chain]
        block = (z - j if up else z + j) * 2 + yy
        src = xn.at[slab(c)] if (j == 0 and chain < col) else xg.at[block, slab(c)]
        at = chain * 6 + (0 if up else 3) + j
        return remote(src, xg.at[block, slab(c)], z_send.at[at], z_recv.at[at], {"seq": s + 2 if up else s - 2})

    def z_arrived(chain, up, j):
        c, yy = chains[chain]
        block = (z - j if up else z + j) * 2 + yy
        at = chain * 6 + (0 if up else 3) + j - 1
        ref = xg.at[block, slab(c)]
        return remote(ref, ref, z_send.at[at], z_recv.at[at], {"seq": s})

    def can(up, j):
        return z >= j if up else z <= 3 - j

    def can_send(up):
        return z < 3 if up else z > 0

    def y_copy(chain, where):
        c = chains[chain][0]
        block = (z + where) * 2 + y
        src = xn.at[slab(c)] if where == 0 else xg.at[block, slab(c)]
        at = chain * 7 + where + 3
        return remote(src, xg.at[block, slab(c)], y_send.at[at], y_recv.at[at], {"seq": other})

    def y_arrived(chain, where):
        c = chains[chain][0]
        ref = xg.at[(z + where) * 2 + 1 - y, slab(c)]
        at = chain * 7 + where + 3
        return remote(ref, ref, y_send.at[at], y_recv.at[at], {"seq": s})

    def start():
        y_copy(col - 1, 0).start()
        for chain in [col - 1] + list(range(col - 1)):
            for up in (True, False):

                @pl.when(can_send(up))
                def _():
                    z_copy(chain, up, 0).start()

            if chain < col - 1:
                y_copy(chain, 0).start()

    def cross_over():
        y_arrived(col - 1, 0).wait_recv()
        for up in (True, False):

            @pl.when(can_send(up))
            def _():
                z_copy(col, up, 0).start()

    def relay(j, chain):
        for up in (True, False):

            @pl.when(can(up, j))
            def _():
                z_arrived(chain, up, j).wait_recv()
                if j < 3:

                    @pl.when(can_send(up))
                    def _():
                        z_copy(chain, up, j).start()

                if chain < col - 1:
                    y_copy(chain, -j if up else j).start()

    def z_round(j):
        for chain in [col - 1] + list(range(col - 1)) + [col]:
            relay(j, chain)

    def finish():
        for chain in range(col - 1):
            y_arrived(chain, 0).wait_recv()
            for j in (1, 2, 3):
                for up in (True, False):

                    @pl.when(can(up, j))
                    def _():
                        y_arrived(chain, -j if up else j).wait_recv()

        y_copy(col - 1, 0).wait_send()
        for chain in range(col - 1):
            y_copy(chain, 0).wait_send()
            for j in (1, 2, 3):
                for up in (True, False):

                    @pl.when(can(up, j))
                    def _():
                        y_copy(chain, -j if up else j).wait_send()

        for chain in range(col + 1):
            for up in (True, False):

                @pl.when(can_send(up))
                def _():
                    z_copy(chain, up, 0).wait_send()

                for j in (1, 2):

                    @pl.when(jnp.logical_and(can(up, j), can_send(up)))
                    def _():
                        z_copy(chain, up, j).wait_send()

    steps = [cross_over] + [functools.partial(z_round, j) for j in (1, 2, 3)]
    return start, steps, finish


def gather_sems(rows):
    col = rows // SLAB
    dma = pltpu.SemaphoreType.DMA
    return [dma(((col + 1) * 6,)), dma(((col + 1) * 6,)), dma((col * 7,)), dma((col * 7,))]


def front_kernel(count, *refs):
    xs, refs = refs[:count], refs[count:]
    wp, pk, gn = refs[:3]
    xgs, refs = refs[3 : 3 + count], refs[3 + count :]
    wg, pg, gg = refs[:3]
    local_sem, w_send, w_recv, d_send, d_recv, p_send, p_recv, g_send, g_recv = refs[3:12]
    sems = [refs[12 + 4 * i : 16 + 4 * i] for i in range(count)]
    s = lax.axis_index("seq")
    d = lax.axis_index("dp")
    n = 8
    cross = lax.rem(d + 2, 4)
    core = d + 1 - 2 * lax.rem(d, 2)
    diag = lax.rem(core + 2, 4)
    peers = [lax.rem(s + k, n) for k in range(1, n)]
    sources = [lax.rem(s + n - 1 - k, n) for k in range(n - 1)] + [s]
    peers_barrier(peers, [cross, core])
    col = pk.shape[0] // SLAB
    gathers = [gather_stages(x, xg, *sm) for x, xg, sm in zip(xs, xgs, sems)]
    own = [
        pltpu.make_async_copy(wp.at[s], wg.at[d, s], local_sem.at[0]),
        pltpu.make_async_copy(pk, pg.at[d], local_sem.at[1]),
        pltpu.make_async_copy(gn, gg.at[d, s], local_sem.at[2]),
    ] + [pltpu.make_async_copy(x, xg.at[s], local_sem.at[3 + i]) for i, (x, xg) in enumerate(zip(xs, xgs))]

    def slab(c):
        return pl.ds(c * SLAB, SLAB)

    def w_copy(k):
        return remote(wp.at[peers[k]], wg.at[d, s], w_send.at[k], w_recv.at[k], {"seq": peers[k]})

    def g_copy(k):
        return remote(gn, gg.at[d, s], g_send.at[k], g_recv.at[k], {"seq": peers[k]})

    def g_over(kind):
        block = cross if kind == 2 else d
        at = 7 + kind
        return remote(gg.at[block], gg.at[block], g_send.at[at], g_recv.at[at], {"dp": cross if kind == 0 else core})

    def d_copy(k, kind):
        block = cross if kind == 2 else d
        src = wp.at[s] if (k == 7 and kind < 2) else wg.at[block, sources[k]]
        at = k * 3 + kind
        return remote(
            src, wg.at[block, sources[k]], d_send.at[at], d_recv.at[at], {"dp": cross if kind == 0 else core}
        )

    def p_copy(c, kind):
        block = cross if kind == 2 else d
        src = pk.at[slab(c)] if kind < 2 else pg.at[block, slab(c)]
        at = c * 3 + kind
        return remote(src, pg.at[block, slab(c)], p_send.at[at], p_recv.at[at], {"dp": cross if kind == 0 else core})

    def arrived(ref, sem_s, sem_r):
        remote(ref, ref, sem_s, sem_r, {"seq": s}).wait_recv()

    def w_relay(k):
        arrived(wg.at[d, sources[k]], w_send.at[k], w_recv.at[k])
        for kind in (0, 1):
            d_copy(k, kind).start()

    def cross_relay(k):
        arrived(wg.at[cross, sources[k]], d_send.at[k * 3], d_recv.at[k * 3])
        d_copy(k, 2).start()

    for k in range(n - 1):
        g_copy(k).start()
    for k in range(n - 1):
        w_copy(k).start()
    gathers[0][0]()
    for kind in (0, 1):
        d_copy(7, kind).start()
    for c in range(col):
        for kind in (0, 1):
            p_copy(c, kind).start()
    for c in own:
        c.start()
    own[2].wait()
    for k in range(n - 1):
        arrived(gg.at[d, sources[k]], g_send.at[k], g_recv.at[k])
    for kind in (0, 1):
        g_over(kind).start()
    steps = gathers[0][1]
    steps[0]()
    steps[1]()
    for k in (0, 1, 5, 6):
        w_relay(k)
    arrived(gg.at[cross], g_send.at[7], g_recv.at[7])
    g_over(2).start()
    steps[2]()
    for k in (2, 3, 4):
        w_relay(k)
    for c in range(col):
        arrived(pg.at[cross, slab(c)], p_send.at[c * 3], p_recv.at[c * 3])
        p_copy(c, 2).start()
    steps[3]()
    for extra in gathers[1:]:
        extra[0]()
    for k in (7, 0, 1, 5, 6, 2, 3, 4):
        cross_relay(k)
    gathers[0][2]()
    for extra in gathers[1:]:
        for st in extra[1]:
            st()
        extra[2]()
    for k in range(n):
        for kind, block in ((1, core), (2, diag)):
            at = k * 3 + kind
            arrived(wg.at[block, sources[k]], d_send.at[at], d_recv.at[at])
    for c in range(col):
        for kind, block in ((1, core), (2, diag)):
            at = c * 3 + kind
            arrived(pg.at[block, slab(c)], p_send.at[at], p_recv.at[at])
    for kind, block in ((1, core), (2, diag)):
        arrived(gg.at[block], g_send.at[7 + kind], g_recv.at[7 + kind])
    for k in range(n - 1):
        w_copy(k).wait_send()
        g_copy(k).wait_send()
    for kind in (0, 1, 2):
        g_over(kind).wait_send()
        for k in range(n):
            d_copy(k, kind).wait_send()
        for c in range(col):
            p_copy(c, kind).wait_send()
    for i, c in enumerate(own):
        if i != 2:
            c.wait()


def front_gather(xs, wp, pk, gn):
    col = pk.shape[0] // SLAB
    count = len(xs)
    dma = pltpu.SemaphoreType.DMA
    scratch = [dma((3 + count,)), dma((7,)), dma((7,)), dma((24,)), dma((24,)), dma((col * 3,)), dma((col * 3,)), dma((10,)), dma((10,))]
    for x in xs:
        scratch += gather_sems(x.shape[0])
    return pl.pallas_call(
        functools.partial(front_kernel, count),
        out_shape=tuple(jax.ShapeDtypeStruct((8,) + x.shape, BF) for x in xs)
        + (
            jax.ShapeDtypeStruct((4,) + wp.shape, BF),
            jax.ShapeDtypeStruct((4,) + pk.shape, BF),
            jax.ShapeDtypeStruct((4, 8) + gn.shape, gn.dtype),
        ),
        in_specs=[pl.BlockSpec(memory_space=pltpu.VMEM)] * (count + 3),
        out_specs=tuple([pl.BlockSpec(memory_space=pl.ANY)] * (count + 3)),
        scratch_shapes=scratch,
        compiler_params=pltpu.CompilerParams(
            collective_id=3, has_side_effects=True, vmem_limit_bytes=60 << 20
        ),
        name="front_gather",
    )(*xs, wp, pk, gn)


def add_blocks(dst, srcs):
    rows = dst.shape[0]
    width = dst.shape[1]
    step = 16 if rows % 16 == 0 else rows

    @pl.loop(0, rows // step)
    def _(i):
        at = pl.ds(pl.multiple_of(i * step, step), step)
        total = srcs[0][at, :].astype(F32)
        for s_ref in srcs[1:]:
            total = total + s_ref[at, :].astype(F32)
        dst[at, :] = total.astype(dst.dtype)


def scatter_stages(part, out, ybuf, zbuf, sbuf, qbuf, y_send, y_recv, z_send, z_recv, q_send, q_recv):
    s = lax.axis_index("seq")
    z, y = s // 2, lax.rem(s, 2)
    other = s + 1 - 2 * y
    rows = out.shape[0]
    slabs = rows // SLAB
    np_ = ybuf.shape[1]
    items = [(c, own, False) for c in range(np_, slabs) for own in (True, False)] + [(c, True, True) for c in range(np_)]

    def own_part(zz, yy, c):
        return part.at[pl.ds(pl.multiple_of((zz * 2 + yy) * rows + c * SLAB, SLAB), SLAB), :]

    def y_at(k):
        return jnp.where(z < 2, 3 - k, k)

    def y_copy(c, k):
        zz = y_at(k)
        at = c * 4 + k
        return remote(own_part(zz, 1 - y, c), ybuf.at[zz, c], y_send.at[at], y_recv.at[at], {"seq": other})

    def base(i, zz):
        c, own, crossed = items[i]
        yy = y if own else 1 - y
        refs = [own_part(zz, yy, c)]
        if crossed:
            refs.append(ybuf.at[zz, c])
        return refs

    def z_at(direction, q, i):
        return (direction * 4 + q) * len(items) + i

    def z_copy(direction, h, q, i):
        zz = q if direction == 0 else 3 - q
        refs = base(i, zz)
        src = refs[0] if (h == 0 and len(refs) == 1) else sbuf.at[direction, q - 1, i]
        at = z_at(direction, q, i)
        return remote(
            src, zbuf.at[direction, q - 1, i], z_send.at[at], z_recv.at[at], {"seq": s + 2 if direction == 0 else s - 2}
        )

    def hop(i, h):
        for direction in (0, 1):
            pos = z if direction == 0 else 3 - z

            @pl.when(pos == h)
            def _():
                for q in range(3, h - 1, -1):
                    if h > 0:
                        z_copy(direction, h, q, i).wait_recv()
                    if q > h:
                        zz = q if direction == 0 else 3 - q
                        refs = base(i, zz)
                        if h > 0:
                            refs = refs + [zbuf.at[direction, q - 1, i]]
                        if len(refs) > 1:
                            add_blocks(sbuf.at[direction, q - 1, i], refs)
                        z_copy(direction, h, q, i).start()

    def q_copy(j):
        return remote(qbuf.at[0, j], qbuf.at[1, j], q_send.at[j], q_recv.at[j], {"seq": other})

    def settle(i):
        c, own, crossed = items[i]
        dst = out.at[pl.ds(c * SLAB, SLAB), :] if own else qbuf.at[0, c - np_]
        for low, high in ((True, False), (False, False), (False, True)):
            where = z == 0 if low else (z == 3 if high else jnp.logical_and(z > 0, z < 3))

            @pl.when(where)
            def _():
                refs = base(i, z)
                if not low:
                    refs = refs + [zbuf.at[0, z - 1, i]]
                if not high:
                    refs = refs + [zbuf.at[1, 2 - z, i]]
                add_blocks(dst, refs)

        if not own:
            q_copy(c - np_).start()

    def start():
        for c in range(np_):
            for k in range(4):
                y_copy(c, k).start()

    def y_wait(i):
        c, own, crossed = items[i]
        if crossed:
            for k in range(4):
                y_copy(c, k).wait_recv()

    steps = []
    for tau in range(len(items) + 4):
        group = []
        for i in range(len(items)):
            h = tau - i
            if 0 <= h <= 4:
                group.append((i, h))

        def step(group=group):
            for i, h in group:
                if h == 0:
                    y_wait(i)
                if h < 4:
                    hop(i, h)
                else:
                    settle(i)

        steps.append(step)

    def finish():
        for c in range(np_, slabs):
            q_copy(c - np_).wait_recv()
            dst = out.at[pl.ds(c * SLAB, SLAB), :]
            add_blocks(dst, [dst, qbuf.at[1, c - np_]])
        for c in range(np_, slabs):
            q_copy(c - np_).wait_send()
        for c in range(np_):
            for k in range(4):
                y_copy(c, k).wait_send()
        for i in range(len(items)):
            for direction in (0, 1):
                pos = z if direction == 0 else 3 - z
                for h in range(3):

                    @pl.when(pos == h)
                    def _():
                        for q in range(3, h, -1):
                            z_copy(direction, h, q, i).wait_send()

    return start, steps, finish


def scatter_scratch(rows, width, np_):
    slabs = rows // SLAB
    nq = slabs - np_
    count = 2 * nq + np_
    dma = pltpu.SemaphoreType.DMA
    return [
        pltpu.VMEM((4, np_, SLAB, width), BF),
        pltpu.VMEM((2, 3, count, SLAB, width), BF),
        pltpu.VMEM((2, 3, count, SLAB, width), BF),
        pltpu.VMEM((2, nq, SLAB, width), BF),
        dma((4 * np_,)),
        dma((4 * np_,)),
        dma((8 * count,)),
        dma((8 * count,)),
        dma((nq,)),
        dma((nq,)),
    ]


def reduce_stages(src, cbuf, abuf, xbuf, c_send, c_recv, x_send, x_recv, blocks, order, settle):
    d = lax.axis_index("dp")
    cross = lax.rem(d + 2, 4)
    core = d + 1 - 2 * lax.rem(d, 2)
    diag = lax.rem(core + 2, 4)

    def c_copy(kind, b):
        at = kind * blocks + b
        return remote(src(diag if kind else core, order(b)), cbuf.at[kind, b], c_send.at[at], c_recv.at[at], {"dp": core})

    def x_copy(b):
        return remote(abuf.at[b], xbuf.at[b], x_send.at[b], x_recv.at[b], {"dp": cross})

    def start():
        for kind in (1, 0):
            for b in range(blocks):
                c_copy(kind, b).start()

    def first(b):
        c_copy(1, b).wait_recv()
        add_blocks(abuf.at[b], [src(cross, order(b)), cbuf.at[1, b]])
        x_copy(b).start()

    def second(b):
        c_copy(0, b).wait_recv()
        x_copy(b).wait_recv()
        settle(b, [src(d, order(b)), cbuf.at[0, b], xbuf.at[b]])

    def finish():
        for b in range(blocks):
            for kind in (0, 1):
                c_copy(kind, b).wait_send()
            x_copy(b).wait_send()

    return start, first, second, finish


def reduce_scratch(blocks, rows, width):
    dma = pltpu.SemaphoreType.DMA
    return [
        pltpu.VMEM((2, blocks, rows, width), BF),
        pltpu.VMEM((blocks, rows, width), BF),
        pltpu.VMEM((blocks, rows, width), BF),
        dma((2 * blocks,)),
        dma((2 * blocks,)),
        dma((blocks,)),
        dma((blocks,)),
    ]


def tail_kernel(count, n_pack, *refs):
    parts, refs = refs[:count], refs[count:]
    g, refs = refs[0], refs[1:]
    pg, refs = (refs[0], refs[1:]) if n_pack else (None, refs)
    outs, refs = refs[:count], refs[count:]
    gout, refs = refs[0], refs[1:]
    pout, refs = (refs[0], refs[1:]) if n_pack else (None, refs)
    scat = [refs[i * 10 : i * 10 + 10] for i in range(count)]
    refs = refs[10 * count :]
    red, refs = refs[:7], refs[7:]
    packed_red, refs = (refs[:7], refs[7:]) if n_pack else (None, refs)
    fbuf, f_send, f_recv = refs
    s = lax.axis_index("seq")
    d = lax.axis_index("dp")
    n = 8
    peers = [lax.rem(s + k, n) for k in range(1, n)]
    peers_barrier(peers, [lax.rem(d + 2, 4), d + 1 - 2 * lax.rem(d, 2)])

    def order(b):
        return lax.rem(s + b, n)

    def f_copy(b):
        return remote(fbuf.at[b - 1], gout.at[s], f_send.at[b - 1], f_recv.at[b - 1], {"seq": order(b)})

    def f_settle(b, srcs):
        if b == 0:
            add_blocks(gout.at[s], srcs)
        else:
            add_blocks(fbuf.at[b - 1], srcs)
            f_copy(b).start()

    scatters = [scatter_stages(p, o, *sc) for p, o, sc in zip(parts, outs, scat)]
    start, first, second, finish = reduce_stages(lambda dd, b: g.at[dd, b], *red, n, order, f_settle)
    for sc in scatters:
        sc[0]()
    start()
    if n_pack:

        def p_settle(b, srcs):
            add_blocks(pout.at[pl.ds(b * SLAB, SLAB), :], srcs)

        p_start, p_first, p_second, p_finish = reduce_stages(
            lambda dd, b: pg.at[dd, pl.ds(b * SLAB, SLAB), :], *packed_red, n_pack, lambda b: b, p_settle
        )
        p_start()
    blocks = [4, 3, 5, 2, 6, 1, 7, 0]
    todo = []
    for b in blocks:
        todo.append(lambda b=b: first(b))
    if n_pack:
        for b in range(n_pack):
            todo.append(lambda b=b: p_first(b))
    seconds = [lambda b=b: second(b) for b in blocks]
    if n_pack:
        seconds = seconds + [lambda b=b: p_second(b) for b in range(n_pack)]
    steps = [st for group in zip(*[sc[1] for sc in scatters]) for st in group]
    if steps:
        steps.pop(0)()
    for t in todo:
        t()
    while steps or seconds:
        if steps:
            steps.pop(0)()
        if seconds:
            seconds.pop(0)()
    for sc in scatters:
        sc[2]()
    for b in range(1, n):
        f_copy(b).wait()
    finish()
    if n_pack:
        p_finish()


def tail_scatter(parts, g, pg, np_):
    rows, width = parts[0].shape[0] // 8 if parts else 0, parts[0].shape[1] if parts else 0
    count = len(parts)
    n_pack = 0 if pg is None else pg.shape[1] // SLAB
    out_shape = [jax.ShapeDtypeStruct((rows, width), F32)] * count + [jax.ShapeDtypeStruct(g.shape[1:], BF)]
    scratch = []
    for _ in range(count):
        scratch += scatter_scratch(rows, width, np_)
    scratch += reduce_scratch(8, g.shape[2], g.shape[3])
    args = list(parts) + [g]
    if n_pack:
        out_shape.append(jax.ShapeDtypeStruct(pg.shape[1:], F32))
        scratch += reduce_scratch(n_pack, SLAB, pg.shape[2])
        args.append(pg)
    scratch += [pltpu.VMEM((7,) + g.shape[2:], BF), pltpu.SemaphoreType.DMA((7,)), pltpu.SemaphoreType.DMA((7,))]
    return pl.pallas_call(
        functools.partial(tail_kernel, count, n_pack),
        out_shape=tuple(out_shape),
        in_specs=[pl.BlockSpec(memory_space=pltpu.VMEM)] * len(args),
        out_specs=tuple([pl.BlockSpec(memory_space=pltpu.VMEM)] * len(out_shape)),
        scratch_shapes=scratch,
        compiler_params=pltpu.CompilerParams(
            collective_id=4, has_side_effects=True, vmem_limit_bytes=63 << 20
        ),
        name="tail_scatter",
    )(*args)


def silu_slope(values_in):
    sigmoid_value = jax.nn.sigmoid(values_in)
    return sigmoid_value * (1.0 + values_in * (1.0 - sigmoid_value))


def dot(a, b, dims):
    return lax.dot_general(a, b, (dims, ((), ())), preferred_element_type=F32)


def segments(length):
    count = max(1, length // SEGMENT)
    size = length // count
    return [(i * size, (i + 1) * size) for i in range(count)]


def forward_scan(step_size, inner, picked, rate2, shard):
    state = rate2.shape[0]
    carry = jnp.zeros(rate2.shape, F32)
    outs, starts = [], []
    for lo, hi in segments(step_size.shape[0]):
        y, start, carry, *gathered = scan_fwd(
            step_size[lo:hi], inner[lo:hi], picked[:, lo:hi], rate2, carry, RANK, state, shard
        )
        outs.append(y)
        starts.append(start)
    return (outs[0] if len(outs) == 1 else jnp.concatenate(outs, axis=0)), starts, gathered


def backward_scan(step_size, inner, grad_scan, picked, rate2, starts, part):
    state = rate2.shape[0]
    carry = jnp.zeros(rate2.shape, F32)
    parts = []
    total = jnp.zeros(rate2.shape, F32)
    spans = segments(step_size.shape[0])
    for (lo, hi), start in reversed(list(zip(spans, starts))):
        s1, s2, decay, gwr, carry, *summed = scan_bwd(
            step_size[lo:hi], inner[lo:hi], grad_scan[lo:hi], picked[:, lo:hi], rate2, start, carry, RANK, state, part
        )
        total = total + decay
        parts.append((s1, s2, gwr))
    parts = parts[::-1]
    if len(parts) == 1:
        s1, s2, gwr = parts[0]
    else:
        s1, s2, gwr = (jnp.concatenate(p, axis=k) for k, p in zip((0, 0, 1), zip(*parts)))
    return s1, s2, gwr, total, summed


def shards(
    block_input,
    norm_gain,
    in_weight,
    conv_weight,
    conv_bias,
    select_weight,
    step_weight,
    step_bias,
    decay_log,
    skip_gain,
    out_weight,
    output_grad,
):
    n_dp, n_seq = lax.axis_size("dp"), lax.axis_size("seq")
    token_rows = block_input[0]
    upstream_rows = output_grad[0]
    width = token_rows.shape[1]
    d_rows = in_weight.shape[0]
    e_rows = out_weight.shape[0]
    local = n_dp * e_rows

    own = token_rows.astype(F32)
    own_scale = lax.rsqrt(jnp.mean(own * own, axis=1, keepdims=True) + EPS)
    pieces = in_weight
    pieces = pieces.reshape(d_rows, 2, n_dp, n_seq, e_rows).transpose(3, 0, 1, 2, 4).reshape(n_seq, d_rows, 2 * local)

    smalls = [select_weight, step_weight, decay_log, conv_weight, conv_bias[:, None], step_bias[:, None], skip_gain[:, None]]
    used = sum(s.shape[1] for s in smalls)
    pad = -used % 128
    packed = jnp.concatenate([out_weight] + smalls + [jnp.zeros((e_rows, pad), BF)], axis=1)
    kernels = (n_dp, n_seq) == (4, 8)
    hide = kernels and HIDE
    if kernels:
        gain_tile = jnp.broadcast_to(jnp.pad(norm_gain.astype(F32), (0, 128 - d_rows))[None], (8, 128))
        *gathered, in_w, packed, gains = front_gather(
            [token_rows] if hide else [token_rows, upstream_rows], pieces, packed, gain_tile
        )
        x = gathered[0]
        packed = packed.reshape(local, packed.shape[2])
        gain = gains[:, :, 0, :d_rows].reshape(width)
    else:
        x = lax.all_gather(token_rows, "seq")
        gathered = [x, lax.all_gather(upstream_rows, "seq")]
        in_w = lax.all_gather(lax.all_to_all(pieces, "seq", 0, 0), "dp")
        packed = lax.all_gather(packed, "dp", axis=0, tiled=True)
        gain = lax.all_gather(norm_gain, ("dp", "seq"), axis=0, tiled=True).astype(F32)
    length = n_seq * token_rows.shape[0]
    in_w = in_w.reshape(width, 2 * local)
    xf = x.reshape(length, width).astype(F32)
    row_scale = lax.rsqrt(jnp.mean(xf * xf, axis=1, keepdims=True) + EPS)
    normed = (xf * row_scale * gain).astype(BF)
    cuts = []
    begin = 0
    for s in [out_weight] + smalls:
        cuts.append((begin, begin + s.shape[1]))
        begin += s.shape[1]
    out_w, sel_w, step_w, dec_w, conv_w, conv_b, step_b, skip = (packed[:, a:b] for a, b in cuts)
    conv_taps = conv_w.astype(F32).T
    conv_b, step_b, skip = (v[:, 0].astype(F32) for v in (conv_b, step_b, skip))
    decay_rate = -jnp.exp(dec_w.astype(F32).T)
    rate2 = decay_rate * (1.0 / LN2)

    mixed = dot(normed, in_w, ((1,), (0,))).astype(BF)
    padded = jnp.concatenate([jnp.zeros((KERNEL - 1, local), BF), mixed[:, :local]], axis=0).astype(F32)
    gate_in = mixed[:, local:].astype(F32)
    conv_out = conv_b + jnp.zeros((length, local), F32)
    for offset in range(KERNEL):
        conv_out = conv_out + padded[offset : offset + length] * conv_taps[offset]
    inner = jax.nn.silu(conv_out).astype(BF)
    inner_f = inner.astype(F32)
    picked = sum_over_seq(dot(sel_w, inner, ((0,), (1,))).astype(BF), n_seq, "sum_picked", 1)
    step_in = picked[:RANK]
    step_raw = dot(step_in, step_w, ((0,), (1,))) + step_b
    step_size = jax.nn.softplus(step_raw)
    scanned, starts, more = forward_scan(step_size, inner_f, picked, rate2, upstream_rows if hide else None)
    mamba_out = scanned + skip * inner_f
    gate_act = jax.nn.silu(gate_in)
    gated_out = (mamba_out * gate_act).astype(BF)
    out_part = dot(gated_out, out_w, ((1,), (0,))).astype(BF)

    upstream = (more[0] if hide else gathered[1]).reshape(length, width)
    grad_gated = dot(upstream, out_w, ((1,), (1,)))
    grad_out_w = dot(gated_out, upstream, ((0,), (0,)))
    grad_scan = grad_gated * gate_act
    grad_gate = grad_gated * mamba_out * silu_slope(gate_in)
    grad_skip = jnp.sum(grad_scan * inner_f, axis=0)
    s1, s2, grad_wr, grad_decay, more = backward_scan(
        step_size, inner_f, grad_scan, picked, rate2, starts, out_part if hide else None
    )
    grad_raw_f = (s1 * LN2 + inner_f * s2) * jax.nn.sigmoid(step_raw)
    grad_step_b = jnp.sum(grad_raw_f, axis=0)
    grad_raw = grad_raw_f.astype(BF)
    grad_step_w = dot(grad_raw, step_in, ((0,), (1,)))
    part = jnp.concatenate([dot(step_w, grad_raw, ((0,), (1,))), grad_wr], axis=0).astype(BF)
    grad_picked = sum_over_seq(part, n_seq, "sum_grad_picked", 2)
    grad_sel = dot(inner, grad_picked, ((0,), (1,)))
    grad_inner = step_size * s2 + grad_scan * skip + dot(grad_picked, sel_w, ((0,), (1,)))
    grad_conv = grad_inner * silu_slope(conv_out)
    grad_conv_b = jnp.sum(grad_conv, axis=0)
    grad_taps = [jnp.sum(grad_conv * padded[k : k + length], axis=0) for k in range(KERNEL)]
    extended = jnp.concatenate([grad_conv, jnp.zeros((KERNEL - 1, local), F32)], axis=0)
    grad_conv_in = jnp.zeros((length, local), F32)
    for k in range(KERNEL):
        grad_conv_in = grad_conv_in + extended[KERNEL - 1 - k : KERNEL - 1 - k + length] * conv_taps[k]
    grad_mixed = jnp.concatenate([grad_conv_in, grad_gate], axis=1).astype(BF)
    grad_in_w = dot(normed, grad_mixed, ((0,), (0,)))
    grad_normed = dot(grad_mixed, in_w, ((1,), (1,)))

    small_grads = [grad_sel, grad_step_w, (grad_decay * decay_rate).T, jnp.stack(grad_taps, axis=1), grad_conv_b[:, None], grad_step_b[:, None], grad_skip[:, None]]
    packed_grad = jnp.concatenate([grad_out_w] + small_grads + [jnp.zeros((local, pad), F32)], axis=1).astype(BF)
    grad_in_w = grad_in_w.astype(BF)
    grad_normed = grad_normed.astype(BF)
    if kernels:
        parts = [grad_normed] if hide else [grad_normed, out_part]
        *summed, grad_in_all, packed_grad = tail_scatter(
            parts,
            grad_in_w.reshape(n_dp, n_seq, d_rows, 2 * local),
            packed_grad.reshape(n_dp, e_rows, packed_grad.shape[1]),
            2,
        )
        grad_normed = summed[0]
        out_rows = more[0] if hide else summed[1]
    else:
        packed_grad = lax.psum_scatter(packed_grad, "dp", scatter_dimension=0, tiled=True).astype(F32)
        grad_in_all = lax.psum_scatter(grad_in_w, "dp", scatter_dimension=0, tiled=True)
        grad_in_all = lax.all_to_all(grad_in_all, "seq", split_axis=0, concat_axis=0, tiled=True)
        grad_in_all = grad_in_all.reshape(n_seq, d_rows, 2 * local)
        grad_normed = lax.psum_scatter(grad_normed, "seq", scatter_dimension=0, tiled=True).astype(F32)
        out_rows = lax.psum_scatter(out_part, "seq", scatter_dimension=0, tiled=True)
    layer_out = (own + out_rows.astype(F32)).astype(BF)
    g_out, g_sel, g_step, g_dec, g_conv, g_cb, g_sb, g_skip = (packed_grad[:, a:b] for a, b in cuts)
    g_in = (
        grad_in_all.reshape(n_seq, d_rows, 2, n_dp, e_rows)
        .transpose(1, 2, 3, 0, 4)
        .reshape(in_weight.shape)
        .astype(F32)
    )
    g_gain = jnp.sum(g_in * in_weight.astype(F32), axis=1) / norm_gain.astype(F32)

    scaled = grad_normed * gain
    grad_rows = own_scale * scaled - own * (own_scale * own_scale * own_scale) * jnp.mean(scaled * own, axis=1, keepdims=True)
    input_grad = (upstream_rows.astype(F32) + grad_rows).astype(BF)
    return (
        layer_out[None],
        input_grad[None],
        g_gain,
        g_in,
        g_conv,
        g_cb[:, 0],
        g_sel,
        g_step,
        g_sb[:, 0],
        g_dec,
        g_skip[:, 0],
        g_out,
    )


def solution(mesh):
    rows = P(("dp", "seq"))
    both = P(("dp", "seq"), None)
    acts = P("dp", "seq", None)
    return jax.shard_map(
        shards,
        mesh=mesh,
        in_specs=(acts, rows, both, both, rows, both, both, rows, both, rows, both, acts),
        out_specs=(acts, acts, rows, both, both, rows, both, both, rows, both, rows, both),
        check_vma=False,
    )
```

time: 629 us -> 467 us (0.74)
  waiting for transfers between devices: 273 us -> 0 us
  Pallas kernels: 195 us -> 343 us
  between operations: 14.8 us -> 1.53 us
  local copies, waits for them, and re-layouts: 43.6 us -> 33.2 us
  matrix products: 57.3 us -> 50.7 us
  starting transfers between devices: 6.48 us -> 0 us
    reduce_scatter x4 -> x0, waiting for transfers between devices: 220 us -> none  [the longest x1 90.2 us: shards(): lax.psum_scatter(out_part, 'seq', scatter_dimension=0, tiled=True)]
    pallas_call x3 -> x4, Pallas kernels: 154 us -> 304 us  [the longest x1 98.9 us: scan_bwd(): pl.pallas_call(functools.partial(bwd_kernel, chunk, lw, ng, rank, state,...]
    all_gather x1 -> x0, waiting for transfers between devices: 52.5 us -> none  [shards(): upstream = lax.all_gather(upstream_rows, 'seq', axis=0, tiled=True)]
    unnamed x102 -> x88, local copies, waits for them, and re-layouts: 17.5 us -> 8.94 us
    dot_general x12, matrix products: 57.3 us -> 50.7 us  [dot(): return lax.dot_general(a, b, (dims, ((), ())), preferred_element_type=F32)]
  transfers between devices with their start and end apart: 6 -> 0, of which waited for: 5 -> 0; matrix products, arithmetic and copies ran while one was open for 9% -> 0% of each run, Pallas kernels for 0% -> 0%
where the time goes in v2:
time: 467 us; the launch traced here: 460 us
  Pallas kernels  343 us (73%)
  matrix products  50.7 us (11%)
  local copies, waits for them, and re-layouts  33.2 us (7%)
  other arithmetic  31.8 us (7%)
    pallas_call x1, Pallas kernels, scan_bwd(): pl.pallas_call(functools.partial(bwd_kernel, chunk, lw, ng, rank, state,...  98.9 us
    pallas_call x1, Pallas kernels, tail_scatter(): pl.pallas_call(functools.partial(tail_kernel, count, n_pack), out_shape=t...  84.5 us
    pallas_call x1, Pallas kernels, front_gather(): pl.pallas_call(functools.partial(front_kernel, count), out_shape=tuple((j...  70.6 us
    dot_general x12, matrix products, dot(): return lax.dot_general(a, b, (dims, ((), ())), preferred_element_type=F32)  50.7 us
    pallas_call x1, Pallas kernels, scan_fwd(): pl.pallas_call(functools.partial(fwd_kernel, chunk, lw, ng, rank, state,...  50.2 us
    pallas_call x2, Pallas kernels, sum_over_seq(): pl.pallas_call(functools.partial(sum_kernel, n), out_shape=jax.ShapeDtype...  38.6 us

profile of v2, /device:TPU:12, one launch (start us, length us, event | category | flops | bytes accessed | tf_op | source)
XLA Modules:
  0.0 459.9 jit_solution(13311670023725998412)
XLA Ops:
  0.7 0.7 pad.6
  1.4 0.6 broadcast_in_dim.20.refs_3_
  2.0 0.8 copy.42
  2.8 0.8 copy.43
  3.6 0.8 copy.44
  4.4 0.8 copy.41
  5.2 0.8 copy.45
  6.0 0.9 copy.40
  6.9 1.9 concatenate.42.refs_2_
  8.8 0.3 copy.71
  9.1 0.4 copy.80
  9.5 1.5 reshape.152.refs_1_
  11.0 70.6 %front_gather.1 = (bf16[8,128,2048]{2,1,0:T(8,128)(2,1)}, bf16[4,8,64,1024]{3,2,1,0:T(8,128)(2,1)}, bf16[4,128,2432]{2,1,0:T(8,128)(2,1)}, f32[4,8,8,128]{3,2,1,0:T(8,128)}) custom-call(bf16[128,2048]{1,0:T(8,128)(2,1)} %bitcast.100, bf16[8,64,1024]{2,1,0:T(8,128)(2,1)} %reshape.152.refs_1_, bf16[128,2432]{1,0:T(8,128)(2,1)} %concatenate.42.refs_2_, ...), custom_call_target="tpu_custom_call" | custom-call | tf_op jit(solution)/shard_map/front_gather/pallas_call | solution.py:727
  81.7 3.1 multiply_reduce_fusion
  84.8 0.9 slice_reduce_fusion.3
  85.8 1.0 slice.146
  86.9 0.6 copy-done.21
  87.5 0.6 bitcast_multiply_fusion.2.refs_3_.refs_4_
  88.1 1.0 slice_convert_fusion.2
  89.3 1.4 slice_convert_fusion
  91.1 5.3 %fusion.1 = bf16[1024,2048]{1,0:T(8,128)(2,1)} fusion(f32[2048]{0:T(1024)S(1)} %mul.243, f32[1024]{0:T(1024)S(1)} %get-tuple-element.99, bf16[8,128,2048]{2,1,0:T(8,128)(2,1)} %get-tuple-element.28), kind=kLoop, calls=%fused_computation.2 | loop fusion | flops 8388608 | bytes 8400896 | tf_op jit(solution)/shard_map/convert_element_type | solution.py:1161
  96.4 1.0 multiply_convert_fusion
  97.5 1.2 copy-done.34
  98.6 4.9 %convolution_convert_fusion.4 = bf16[1024,1024]{1,0:T(8,128)(2,1)S(1)} fusion(bf16[1024,2048]{1,0:T(8,128)(2,1)S(1)} %bitcast.101, bf16[2048,1024]{1,0:T(8,128)(2,1)S(1)} %bitcast.145), kind=kOutput, calls=%fused_computation.38 | convolution fusion | flops 4296015872 | bytes 10485760 | tf_op jit(solution)/shard_map/dot_general | solution.py:1068
  103.6 1.2 copy-done.17
  104.8 0.3 pad_convert_fusion
  105.2 3.3 fusion.39
  108.5 2.3 convolution_convert_fusion.5.part_ref
  110.9 20.4 %sum_picked.1.refs_2_.refs_3_ = bf16[160,1024]{1,0:T(8,128)(2,1)} custom-call(bf16[160,1024]{1,0:T(8,128)(2,1)} %convolution_convert_fusion.5.part_ref), custom_call_target="tpu_custom_call" | custom-call | tf_op jit(solution)/shard_map/sum_picked/pallas_call | solution.py:447
  131.3 4.4 compare_select_fusion
  135.7 0.6 broadcast_6_refs_4__refs_6_.2.refs_4_.refs_6_
  136.3 50.2 %scan_fwd.1 = (f32[1024,512]{1,0:T(8,128)}, f32[16,8,512]{2,1,0:T(8,128)}, f32[16,512]{1,0:T(8,128)}, bf16[8,128,2048]{2,1,0:T(8,128)(2,1)}) custom-call(f32[1024,512]{1,0:T(8,128)} %get-tuple-element.103.refs_0_, f32[1024,512]{1,0:T(8,128)} %get-tuple-element.82.refs_1_, bf16[160,1024]{1,0:T(8,128)(2,1)} %sum_picked.1.refs_2_.refs_3_, ...), custom_call_target="tpu_custom_call" | custom-call | tf_op jit(solution)/shard_map/scan_fwd/pallas_call | solution.py:191
  186.5 8.8 %fusion.8 = (bf16[1024,512]{1,0:T(8,128)(2,1)}, bf16[1024,512]{1,0:T(8,128)(2,1)S(1)}, bf16[512]{0:T(512)(128)(2,1)S(1)}, f32[1024,512]{1,0:T(8,128)}) fusion(f32[1024,512]{1,0:T(8,128)} %get-tuple-element.33, bf16[1024,512]{1,0:T(8,128)(2,1)S(1)} %get-tuple-element.83, f32[512]{0:T(512)S(1)} %bitcast.139, bf16[1024,1024]{1,0:T(8,128)(2,1)} %copy-done.17, ...), kind=kOutput, calls=%fused_computation.19 | convolution fusion | flops 2157968896 | bytes 14683136 | tf_op jit(solution)/shard_map/dot_general | solution.py:1068
  195.2 0.8 copy.56
  196.0 0.5 copy.62
  196.6 6.0 %convolution_convert_fusion.3 = bf16[4,128,2048]{2,1,0:T(8,128)(2,1)} fusion(bf16[4,128,1024]{2,1,0:T(8,128)(2,1)S(1)} %bitcast.109, bf16[1024,2048,1]{1,0,2:T(8,128)(2,1)} %bitcast.148), kind=kOutput, calls=%fused_computation.12 | convolution fusion | flops 2148532224 | bytes 7340032 | tf_op jit(solution)/shard_map/dot_general | solution.py:1068
  202.6 4.3 convolution_convert_fusion.refs_7_
  206.9 98.9 %scan_bwd.1 = (f32[1024,512]{1,0:T(8,128)}, f32[1024,512]{1,0:T(8,128)}, f32[16,512]{1,0:T(8,128)}, f32[32,1024]{1,0:T(8,128)}, f32[16,512]{1,0:T(8,128)}, /*index=5*/f32[128,2048]{1,0:T(8,128)}) custom-call(f32[1024,512]{1,0:T(8,128)} %get-tuple-element.103.refs_0_, f32[1024,512]{1,0:T(8,128)} %get-tuple-element.82.refs_1_, ...), custom_call_target="tpu_custom_call" | custom-call | tf_op jit(solution)/shard_map/scan_bwd/pallas_call | solution.py:375
  305.8 0.8 fusion.33
  306.6 4.1 fusion.38
  310.8 1.1 convolution_convert_fusion.8
  312.2 1.5 convolution_convert_fusion.6
  313.8 0.7 pad_maximum_fusion.3.part_ref
  314.6 18.2 %sum_grad_picked.1 = bf16[160,1024]{1,0:T(8,128)(2,1)} custom-call(bf16[160,1024]{1,0:T(8,128)(2,1)} %pad_maximum_fusion.3.part_ref), custom_call_target="tpu_custom_call" | custom-call | tf_op jit(solution)/shard_map/sum_grad_picked/pallas_call | solution.py:447
  332.8 4.2 multiply_multiply_fusion
  337.2 2.0 multiply_reduce_fusion.3
  339.2 0.3 convolution_convert_fusion.7
  340.0 6.4 %convolution_convert_fusion.1 = bf16[2048,1024]{1,0:T(8,128)(2,1)} fusion(bf16[1024,2048]{1,0:T(8,128)(2,1)S(1)} %copy-done.8, bf16[1024,512]{1,0:T(8,128)(2,1)S(1)} %copy-done.37, bf16[1024,512]{1,0:T(8,128)(2,1)S(1)} %get-tuple-element.92), kind=kOutput, calls=%fused_computation.7 | convolution fusion | flops 4301258752 | bytes 10485760 | tf_op jit(solution)/shard_map/dot_general | solution.py:1068
  346.4 6.3 %convolution_convert_fusion.2.refs_0_ = bf16[1024,2048]{1,0:T(8,128)(2,1)} fusion(bf16[2048,1024]{1,0:T(8,128)(2,1)S(1)} %bitcast.146, bf16[1024,512]{1,0:T(8,128)(2,1)S(1)} %copy-done.37, bf16[1024,512]{1,0:T(8,128)(2,1)S(1)} %get-tuple-element.92), kind=kOutput, calls=%fused_computation.8 | convolution fusion | flops 4301258752 | bytes 10485760 | tf_op jit(solution)/shard_map/dot_general | solution.py:1068
  353.9 0.7 broadcast_in_dim.22
  354.5 5.6 %concatenate.57.refs_2_ = bf16[4,128,2432]{2,1,0:T(8,128)(2,1)} concatenate(bf16[4,128,2048]{2,1,0:T(8,128)(2,1)S(1)} %copy-done.12, bf16[4,128,160]{2,1,0:T(8,128)(2,1)S(1)} %bitcast.107, bf16[4,128,128]{2,1,0:T(8,128)(2,1)} %bitcast.120, bf16[4,128,16]{2,1,0:T(8,128)(2,1)S(1)} %bitcast.110, bf16[4,128,1]{2,1,0:T(8,128)(2,1)S(1)} %copy.50, bf16[4,128,1]{2,1,0:T(8,128)(2,1)S(1)} %copy.51, ...), dimensions={2} | concatenate | bytes 4980736 | tf_op jit(solution)/shard_map/concatenate | solution.py:1220
  360.2 84.5 %tail_scatter.1 = (f32[128,2048]{1,0:T(8,128)}, bf16[8,64,1024]{2,1,0:T(8,128)(2,1)}, f32[128,2432]{1,0:T(8,128)}) custom-call(bf16[1024,2048]{1,0:T(8,128)(2,1)} %convolution_convert_fusion.2.refs_0_, bf16[4,8,64,1024]{3,2,1,0:T(8,128)(2,1)} %bitcast.105, bf16[4,128,2432]{2,1,0:T(8,128)(2,1)} %concatenate.57.refs_2_), custom_call_target="tpu_custom_call" | custom-call | tf_op jit(solution)/shard_map/tail_scatter/pallas_call | solution.py:1049
  444.7 1.6 fusion.14
  446.3 3.0 fusion.21
  449.3 0.7 slice_reduce_fusion
  450.1 0.7 copy.60
  450.8 0.7 slice.127
  451.6 0.7 copy.58
  452.2 1.1 slice.131
  453.3 0.7 copy.59
  454.1 0.9 reshape.162
  455.0 1.2 copy.57
  456.3 2.9 multiply_reduce_fusion.1
  459.2 0.5 convert_divide_fusion
  (96 shorter events, 2.9 us)
Async XLA Ops:
  0.6 8.1 %copy-start.9 = (bf16[64,8192]{1,0:T(8,128)(2,1)S(1)}, bf16[64,8192]{1,0:T(8,128)(2,1)}, u32[]{:S(2)}) copy-start(bf16[64,8192]{1,0:T(8,128)(2,1)} %param.14) | copy-start | bytes 3145732
  85.8 10.6 %copy-start.19 = (f32[2048]{0:T(1024)}, f32[2048]{0:T(1024)S(1)}, u32[]{:S(2)}) copy-start(f32[2048]{0:T(1024)S(1)} %mul.243) | copy-start | bytes 24580
  86.9 0.6 copy-start.21
  89.3 15.9 %copy-start.23 = (f32[1,512]{1,0:T(1,128)}, f32[1,512]{1,0:T(1,128)S(1)}, u32[]{:S(2)}) copy-start(f32[1,512]{1,0:T(1,128)S(1)} %get-tuple-element.95) | copy-start | bytes 6148
  89.3 15.9 %copy-start.25 = (f32[1,512]{1,0:T(1,128)}, f32[1,512]{1,0:T(1,128)S(1)}, u32[]{:S(2)}) copy-start(f32[1,512]{1,0:T(1,128)S(1)} %get-tuple-element.96) | copy-start | bytes 6148
  89.3 15.9 %copy-start.27 = (f32[1,512]{1,0:T(1,128)}, f32[1,512]{1,0:T(1,128)S(1)}, u32[]{:S(2)}) copy-start(f32[1,512]{1,0:T(1,128)S(1)} %get-tuple-element.97) | copy-start | bytes 6148
  89.3 15.9 %copy-start.29 = (f32[1,512]{1,0:T(1,128)}, f32[1,512]{1,0:T(1,128)S(1)}, u32[]{:S(2)}) copy-start(f32[1,512]{1,0:T(1,128)S(1)} %get-tuple-element.98) | copy-start | bytes 6148
  90.8 95.6 %copy-start.32 = (f32[512,1]{0,1:T(1,128)}, f32[512,1]{0,1:T(1,128)S(1)}, u32[]{:S(2)}) copy-start(f32[512,1]{0,1:T(1,128)S(1)} %copy.76) | copy-start | bytes 6148
  91.0 40.3 %copy-start.31 = (f32[512,1]{0,1:T(1,128)}, f32[512,1]{0,1:T(1,128)S(1)}, u32[]{:S(2)}) copy-start(f32[512,1]{0,1:T(1,128)S(1)} %copy.75) | copy-start | bytes 6148
  91.1 5.3 %copy-start.2 = (bf16[8,128,2048]{2,1,0:T(8,128)(2,1)S(1)}, bf16[8,128,2048]{2,1,0:T(8,128)(2,1)}, u32[]{:S(2)}) copy-start(bf16[8,128,2048]{2,1,0:T(8,128)(2,1)} %get-tuple-element.28) | copy-start | bytes 12582916
  96.4 2.2 copy-start.34
  103.5 1.3 copy-start.17
  105.2 3.3 copy-start
  108.5 77.9 %copy-start.3 = (bf16[1024,512]{1,0:T(8,128)(2,1)}, bf16[1024,512]{1,0:T(8,128)(2,1)S(1)}, u32[]{:S(2)}) copy-start(bf16[1024,512]{1,0:T(8,128)(2,1)S(1)} %get-tuple-element.83) | copy-start | bytes 3145732
  196.6 6.0 %copy-start.18 = (bf16[4,128,2432]{2,1,0:T(8,128)(2,1)S(1)}, bf16[4,128,2432]{2,1,0:T(8,128)(2,1)}, u32[]{:S(2)}) copy-start(bf16[4,128,2432]{2,1,0:T(8,128)(2,1)} %get-tuple-element.27) | copy-start | bytes 7471108
  306.6 4.1 copy-start.11
  306.6 5.3 %copy-start.22 = (f32[32,1024]{1,0:T(8,128)S(1)}, f32[32,1024]{1,0:T(8,128)}, u32[]{:S(2)}) copy-start(f32[32,1024]{1,0:T(8,128)} %get-tuple-element.37) | copy-start | bytes 393220
  310.8 22.0 %copy-start.5 = (f32[1024,512]{1,0:T(8,128)S(1)}, f32[1024,512]{1,0:T(8,128)}, u32[]{:S(2)}) copy-start(f32[1024,512]{1,0:T(8,128)} %get-tuple-element.103.refs_0_) | copy-start | bytes 6291460
  310.8 22.0 %copy-start.33 = (f32[512,1]{0,1:T(1,128)S(1)}, f32[512,1]{0,1:T(1,128)}, u32[]{:S(2)}) copy-start(f32[512,1]{0,1:T(1,128)} %copy-done.32) | copy-start | bytes 6148
  332.8 4.3 copy-start.1
  332.8 4.3 copy-start.24
  332.8 4.3 copy-start.26
  332.8 4.3 copy-start.28
  332.8 4.3 copy-start.30
  337.1 2.1 copy-start.4
  337.2 2.1 copy-start.14
  337.2 2.6 copy-start.8
  337.2 2.9 copy-start.37
  340.0 6.4 %copy-start.35 = (bf16[4,8,64,1024]{3,2,1,0:T(8,128)(2,1)S(1)}, bf16[4,8,64,1024]{3,2,1,0:T(8,128)(2,1)}, u32[]{:S(2)}) copy-start(bf16[4,8,64,1024]{3,2,1,0:T(8,128)(2,1)} %get-tuple-element.30) | copy-start | bytes 12582916
  346.4 8.1 %copy-start.12 = (bf16[4,128,2048]{2,1,0:T(8,128)(2,1)S(1)}, bf16[4,128,2048]{2,1,0:T(8,128)(2,1)}, u32[]{:S(2)}) copy-start(bf16[4,128,2048]{2,1,0:T(8,128)(2,1)} %convolution_convert_fusion.3) | copy-start | bytes 6291460
  346.4 8.1 %copy-start.16 = (bf16[4,128,1]{2,1,0:T(8,128)(2,1)S(1)}, bf16[4,128,1]{2,1,0:T(8,128)(2,1)}, u32[]{:S(2)}) copy-start(bf16[4,128,1]{2,1,0:T(8,128)(2,1)} %copy.56) | copy-start | bytes 3076
  360.2 84.5 %copy-start.6 = (bf16[1,128,2048]{2,1,0:T(8,128)(2,1)S(1)}, bf16[1,128,2048]{2,1,0:T(8,128)(2,1)}, u32[]{:S(2)}) copy-start(bf16[1,128,2048]{2,1,0:T(8,128)(2,1)} %param.12) | copy-start | bytes 1572868
  360.2 84.5 %copy-start.20 = (f32[2048]{0:T(1024)S(1)}, f32[2048]{0:T(1024)}, u32[]{:S(2)}) copy-start(f32[2048]{0:T(1024)} %copy-done.19) | copy-start | bytes 24580
  444.6 1.6 copy-start.7
  446.3 3.0 copy-start.13
  449.3 4.8 %copy-start.15 = (bf16[8,64,1024]{2,1,0:T(8,128)(2,1)S(1)}, bf16[8,64,1024]{2,1,0:T(8,128)(2,1)}, u32[]{:S(2)}) copy-start(bf16[8,64,1024]{2,1,0:T(8,128)(2,1)} %get-tuple-element.40) | copy-start | bytes 3145732
  455.0 1.2 copy-start.10
  456.3 2.9 copy-start.36
